TPU v7x, 128 devices: a whole 4x4x4 slice. The times are simulated.
128 devices in a mesh: grp: 8 (over y, x_lo), slab: 16 (over z, x_hi, core).
Axes of the slice: x: 4 (x_hi: 2, x_lo: 2; x = x_hi * 2 + x_lo), y: 4, z: 4, core: 2. Of those that a mesh axis runs over, the one named last changes fastest.
Arguments:
- forcing: float32 [8, 3, 128, 128, 128], P('grp', None, 'slab'), may hold values from -18 to 18
- stiffness: float32 [8, 3, 128, 128, 128], P('grp', None, 'slab'), may hold values from 0.25 to 4
- anisotropy: float32 [8, 3, 3], P('grp'), may hold values from 0.3 to 3
- coupling: float32 [8, 3, 3], P('grp'), may hold values from -0.3 to 2, as said below
- levels: int32 [8, 2], replicated, may hold values from 0 to 2
- neighbours: int32 [8, 3], replicated, may hold values from -1 to 7, as said below
Outputs:
- mixed: float32 [8, 3, 128, 128, 128], P('grp', None, 'slab')
Inputs may be any that keep to these rules, and one draw needn't show every extreme that they name: neighbours[g, 0], [g, 1], [g, 2] name a pair whose levels are those of pair g less (1, 0), (0, 1), (1, 1), or are -1 where no pair has those levels. `coupling`: symmetric; diagonal entries 0.8 to 2, off-diagonal entries at most 0.3 in magnitude.
All inputs are finite; a program needn't handle non-finite values.
Results may differ from a plain program's by a relative error of at most 0.0003.
Values sent between devices are 32-bit elements; how exact they have to be, the bound alone decides.
A program may use at most 64 MiB of HBM per device.

v0:
```python
import jax
import jax.numpy as jnp
from jax import lax
from jax.sharding import Mesh
from jax.sharding import PartitionSpec as P

ITERS = 2
GRP = ("grp_0", "grp_1")


exact_mode = lax.Precision.HIGHEST


def padded_2(shard, sides, width):
    for axis, dim in sides:
        peers, length = (lax.axis_size(axis), shard.shape[dim])
        up = [(i, (i + 1) % peers) for i in range(peers - 1)]
        down = [(j, i) for i, j in up]
        last = lax.slice_in_dim(shard, length - width, length, axis=dim)
        leading = lax.slice_in_dim(shard, 0, width, axis=dim)
        before = lax.ppermute(last, axis, up)
        after = lax.ppermute(leading, axis, down)
        shard = jnp.concatenate([before, shard, after], axis=dim)
    return shard


def copy_for_each(shard, axis):
    copies = jnp.broadcast_to(shard, (lax.axis_size(axis), *shard.shape))
    return lax.all_to_all(copies, axis, split_axis=0, concat_axis=0, tiled=True)


def over_copies(shard, axis):
    everything = copy_for_each(shard, axis)
    return jnp.sum(everything, axis=0)


def own_rows(subtotal, axes):
    for axis in axes:
        subtotal = lax.psum_scatter(subtotal, axis, scatter_dimension=0, tiled=True)
    return subtotal


def level_factor(level_ids):
    return jnp.where(level_ids == 0, 4, jnp.where(level_ids == 1, 2, 1)).astype(jnp.int32)


def pair_shape(levels, pair_ids, width, depth, slabs):
    chosen = jnp.take(levels, pair_ids, axis=0)
    cells_x = width // level_factor(chosen[..., 0])
    run_z = depth // level_factor(chosen[..., 1])
    return (cells_x, run_z, run_z * slabs)


def step_up(values, axis_dim):
    length = values.shape[axis_dim]
    widths = [(0, 0)] * values.ndim
    widths[axis_dim] = (0, 1)
    return lax.slice_in_dim(jnp.pad(values, widths), 1, length + 1, axis=axis_dim)


def step_down(values, axis_dim):
    length = values.shape[axis_dim]
    widths = [(0, 0)] * values.ndim
    widths[axis_dim] = (1, 0)
    return lax.slice_in_dim(jnp.pad(values, widths), 0, length, axis=axis_dim)


def spread_out(totals):
    return totals[:, None, None, None, None]


def with_rims(values, run_z):
    row_index = jnp.arange(values.shape[2], dtype=jnp.int32)
    picking = (row_index[None, :] == run_z[:, None] - 1).astype(jnp.float32)
    last_row = jnp.sum(values * picking[:, None, :, None, None], axis=2)
    stacked = jnp.stack([values[:, :, 0], last_row], axis=2)
    padded = padded_2(stacked, (("slab", 2),), 1)
    return (padded[:, :, 0], padded[:, :, 3])


def z_beside(values, run_z, below_rim, above_rim):
    row_index = jnp.arange(values.shape[2], dtype=jnp.int32)
    above_rows = jnp.concatenate([values[:, :, 1:], jnp.zeros_like(values[:, :, :1])], axis=2)
    at_top = (row_index[None, :] == run_z[:, None] - 1)[:, None, :, None, None]
    above_rows = jnp.where(at_top, above_rim[:, :, None], above_rows)
    below_rows = jnp.concatenate([below_rim[:, :, None], values[:, :, :-1]], axis=2)
    return (above_rows, below_rows)


def operate(values, run_z, face_list, coefficient, coupling, active):
    below_rim, above_rim = with_rims(values, run_z)
    above_rows, below_rows = z_beside(values, run_z, below_rim, above_rim)
    beside = (
        (step_up(values, 4), step_down(values, 4)),
        (step_up(values, 3), step_down(values, 3)),
        (above_rows, below_rows),
    )
    result = jnp.sum(coupling[:, :, :, None, None, None] * values[:, None], axis=2)
    for facing in range(3):
        upper_face, lower_face = face_list[facing]
        result = result + coefficient[:, :, facing, None, None, None] * (
            upper_face * (values - beside[facing][0]) + lower_face * (values - beside[facing][1])
        )
    return result * active


def pair_sums(first, second):
    return jnp.sum(first * second, axis=(1, 2, 3, 4))


def joint_totals(residual, precond, applied):
    return (
        over_copies(pair_sums(residual, precond), "slab"),
        over_copies(pair_sums(precond, applied), "slab"),
    )


def mixing_weights(levels, neighbours, target, sources, width, depth, slabs, slab_index):
    target_x, target_run, target_depth = pair_shape(levels, target, width, depth, slabs)
    source_x, source_run, source_depth = pair_shape(levels, sources, width, depth, slabs)
    link_ids = jnp.take(neighbours, target, axis=0)
    signs = (
        (sources == target).astype(jnp.float32)
        - (sources == link_ids[0]).astype(jnp.float32)
        - (sources == link_ids[1]).astype(jnp.float32)
        + (sources == link_ids[2]).astype(jnp.float32)
    )
    fine_x = jnp.arange(width, dtype=jnp.int32)
    centres_x = fine_x.astype(jnp.float32) + 0.5
    along_x = (
        centres_x[None, :] * (source_x.astype(jnp.float32) / target_x.astype(jnp.float32))[:, None]
    )
    weight_x = jnp.maximum(0.0, 1.0 - jnp.abs(along_x[:, :, None] - centres_x[None, None, :]))
    weight_x = weight_x * (fine_x < target_x).astype(jnp.float32)[None, :, None]
    weight_x = weight_x * (fine_x[None, :] < source_x[:, None]).astype(jnp.float32)[:, None, :]
    fine_z = jnp.arange(depth, dtype=jnp.int32)
    along_z = ((slab_index * target_run + fine_z).astype(jnp.float32) + 0.5)[None, :] * (
        source_depth.astype(jnp.float32) / target_depth.astype(jnp.float32)
    )[:, None]
    columns = jnp.arange(depth + 2, dtype=jnp.int32)
    coarse_ids = slab_index * source_run[:, None] - 1 + columns[None, :]
    coarse_ids = jnp.where(
        columns[None, :] == depth + 1, (slab_index + 1) * source_run[:, None], coarse_ids
    )
    weight_z = jnp.maximum(
        0.0, 1.0 - jnp.abs(along_z[:, :, None] - (coarse_ids.astype(jnp.float32) + 0.5)[:, None, :])
    )
    weight_z = (
        weight_z * (fine_z < target_run).astype(jnp.float32)[None, :, None] * signs[:, None, None]
    )
    return (weight_x, weight_z)


def contribute(pieces, weight_x, weight_z):
    vertical = jnp.einsum("pkn,pcnyx->pckyx", weight_z, pieces, precision=exact_mode)
    return jnp.einsum("pckyx,pmx->ckym", vertical, weight_x, precision=exact_mode)


def per_device(forcing, stiffness, anisotropy, coupling, levels, neighbours):
    own_count = forcing.shape[0]
    depth = forcing.shape[2]
    height = forcing.shape[3]
    width = forcing.shape[4]
    slabs = lax.axis_size("slab")
    slab_index = lax.axis_index("slab")
    own_ids = lax.axis_index(GRP) * own_count + jnp.arange(own_count, dtype=jnp.int32)
    cells_x, run_z, depth_z = pair_shape(levels, own_ids, width, depth, slabs)
    row_index = jnp.arange(depth, dtype=jnp.int32)
    col_index = jnp.arange(width, dtype=jnp.int32)
    active = (
        (row_index[None, :] < run_z[:, None])[:, None, :, None, None]
        & (col_index[None, :] < cells_x[:, None])[:, None, None, None, :]
    ).astype(jnp.float32)
    source = forcing * active
    scales = jnp.stack(
        [
            (cells_x.astype(jnp.float32) / height) ** 2,
            jnp.ones(own_count, jnp.float32),
            (depth_z.astype(jnp.float32) / height) ** 2,
        ],
        axis=1,
    )
    coefficient = anisotropy * scales[:, None, :]
    kept = stiffness * active
    vertical_k = kept[:, 2:3]
    below_k, above_k = with_rims(vertical_k, run_z)
    above_rows_k, below_rows_k = z_beside(vertical_k, run_z, below_k, above_k)
    diagonal = jnp.diagonal(coupling, axis1=1, axis2=2)[:, :, None, None, None]
    face_list = []
    for facing in range(3):
        single = kept[:, facing : facing + 1]
        if facing == 2:
            upper_face = 0.5 * (single + above_rows_k)
            lower_face = 0.5 * (single + below_rows_k)
        else:
            upper_face = 0.5 * (single + step_up(single, 4 - facing))
            lower_face = 0.5 * (single + step_down(single, 4 - facing))
        face_list.append((upper_face, lower_face))
        diagonal = diagonal + coefficient[:, :, facing, None, None, None] * (
            upper_face + lower_face
        )
    solution = jnp.zeros_like(source)
    residual = source
    precond = residual / diagonal
    applied = operate(precond, run_z, face_list, coefficient, coupling, active)
    rz_now, curvature = joint_totals(residual, precond, applied)
    step_size = rz_now / curvature
    search = precond
    along_image = applied
    for iteration in range(ITERS):
        solution = solution + spread_out(step_size) * search
        if iteration + 1 < ITERS:
            residual = residual - spread_out(step_size) * along_image
            precond = residual / diagonal
            applied = operate(precond, run_z, face_list, coefficient, coupling, active)
            rz_next, curvature = joint_totals(residual, precond, applied)
            beta_ratio = rz_next / rz_now
            step_size = rz_next / (curvature - beta_ratio * rz_next / step_size)
            search = precond + spread_out(beta_ratio) * search
            along_image = applied + spread_out(beta_ratio) * along_image
            rz_now = rz_next
    below_rim, above_rim = with_rims(solution, run_z)
    extended = jnp.concatenate([below_rim[:, :, None], solution, above_rim[:, :, None]], axis=2)

    def one_target(target):
        weight_x, weight_z = mixing_weights(
            levels, neighbours, target, own_ids, width, depth, slabs, slab_index
        )
        return contribute(extended, weight_x, weight_z)

    return own_rows(
        lax.map(one_target, jnp.arange(own_count * lax.axis_size(GRP), dtype=jnp.int32)), GRP
    )


def solution(mesh):
    finer = Mesh(mesh.devices.reshape(4, 2, mesh.shape["slab"]), ("grp_0", "grp_1", "slab"))
    placed = (
        P(GRP, None, "slab", None, None),
        P(GRP, None, "slab", None, None),
        P(GRP, None, None),
        P(GRP, None, None),
        P(),
        P(),
    )
    return jax.shard_map(
        per_device,
        mesh=finer,
        in_specs=placed,
        out_specs=P(GRP, None, "slab", None, None),
        check_vma=False,
    )
```

profile of v0, /device:TPU:0, one launch (start us, length us, event | category | flops | bytes accessed | tf_op | source)
XLA Modules:
  0.0 426.0 jit_solution(139615862498638634)
XLA Ops:
  15.9 4.1 collective-permute-done
  25.3 7.0 %collective-permute-start.3 = (f32[1,3,1,128,128]{4,3,2,1,0:T(8,128)S(1)}, f32[1,3,1,128,128]{4,3,2,1,0:T(8,128)S(1)}, u32[]{:S(2)}, u32[]{:S(2)}) collective-permute-start(f32[1,3,1,128,128]{4,3,2,1,0:T(8,128)S(1)} %bitcast.155), channel_id=1, source_target_pairs={{0,1},{1,2},{2,3},{3,4},{4,5},{5,6},{6,7},{7,8},{8,9},{9,10},{10,1... | collective-permute-start | bytes 589832 | tf_op jit(solution)/shard_map/ppermute | solution.py:21
  33.4 3.9 multiply_reduce_fusion.5
  38.0 21.1 %all_to_all.24 = f32[16,1,1]{2,1,0:T(1,128)S(1)} all-to-all(f32[16,1,1]{2,1,0:T(1,128)S(1)} %broadcast_in_dim.201), channel_id=1, replica_groups=mesh['grp_0'=4,'grp_1'=2,'slab'=16] {'slab'}, dimensions={0} | all-to-all | bytes 128 | tf_op jit(solution)/shard_map/all_to_all | solution.py:29
  60.4 3.5 all-to-all-start.1
  64.6 6.7 %all-to-all-done.1 = f32[16,1,1]{2,1,0:T(1,128)S(1)} async-done(((f32[16,1,1]{2,1,0:T(1,128)}), f32[16,1,1]{2,1,0:T(1,128)S(1)}, u32[]{:S(2)}, u32[]{:S(2)}) %all-to-all-start.1) | async-done | bytes 96 | tf_op jit(solution)/shard_map/all_to_all | solution.py:29
  73.1 3.7 multiply_reduce_fusion.3
  80.0 3.4 all-to-all-start.2
  84.7 3.7 collective-permute-start.5
  94.2 4.9 %fusion.82 = f32[]{:T(128)} fusion(f32[1,3,8,128,128]{4,3,2,1,0:T(8,128)S(1)} %get-tuple-element.358, f32[1,3,7,128,128]{4,3,2,1,0:T(8,128)} %get-tuple-element.375, f32[1,3,1,128,128]{4,3,2,1,0:T(8,128)} %collective-permute-done.5, f32[1,3,7,128,128]{4,3,2,1,0:T(8,128)} %get-tuple-element.374, f32[3,8,128,128]{3,2,1,0:T(8,128)} %multiply_reduce_fusion, ...), kind=kLoop, calls=%fused_computation.111 | loop fusion | flops 10223615 | bytes 9441328 | tf_op jit(solution)/shard_map/reduce_sum | solution.py:108
  100.2 8.9 %all-to-all-start.3 = ((f32[16,1,1]{2,1,0:T(1,128)}), f32[16,1,1]{2,1,0:T(1,128)S(1)}, u32[]{:S(2)}, u32[]{:S(2)}) async-start(f32[16,1,1]{2,1,0:T(1,128)} %broadcast_in_dim.209), calls=%async_computation.3 | async-start | bytes 16384 | tf_op jit(solution)/shard_map/all_to_all | solution.py:29
  109.9 6.7 %all-to-all-done.3 = f32[16,1,1]{2,1,0:T(1,128)S(1)} async-done(((f32[16,1,1]{2,1,0:T(1,128)}), f32[16,1,1]{2,1,0:T(1,128)S(1)}, u32[]{:S(2)}, u32[]{:S(2)}) %all-to-all-start.3) | async-done | bytes 96 | tf_op jit(solution)/shard_map/all_to_all | solution.py:29
  121.5 3.2 collective-permute-start.6
  130.0 121.3 %while.16 = (s32[]{:T(128)}, f32[8,3,8,128,128]{4,3,2,1,0:T(8,128)}, s32[8]{0:T(128)S(1)}, s32[8,2]{0,1:T(2,128)S(1)}, s32[]{:T(128)}, /*index=5*/f32[1]{0:T(128...) while((s32[]{:T(128)}, ...), condition=%wide.region_15.17_spmd, body=%wide.region_14.16_spmd.sunk | while | flops 651265536 | bytes 6690302 | solution.py:232
  137.6 3.5 fusion.123
  152.8 3.5 fusion.123
  168.0 3.5 fusion.123
  183.1 3.5 fusion.123
  198.3 3.5 fusion.123
  213.4 3.5 fusion.123
  228.6 3.5 fusion.123
  243.8 3.5 fusion.123
  251.4 119.8 %reduce-scatter.3.cloned.1.call-done = f32[2,3,8,128,128]{4,3,2,1,0:T(8,128)} async-done(((f32[8,3,8,128,128]{4,3,2,1,0:T(8,128)}), f32[2,3,8,128,128]{4,3,2,1,0:T(8,128)}) %reduce-scatter.3.cloned.1.call-update) | async-done | bytes 3145744 | tf_op jit(solution)/shard_map/reduce_scatter | solution.py:39
  371.2 48.0 %reduce-scatter.5.cloned.1.call-done = f32[1,3,8,128,128]{4,3,2,1,0:T(8,128)} async-done(((f32[2,3,8,128,128]{4,3,2,1,0:T(8,128)}), f32[1,3,8,128,128]{4,3,2,1,0:T(8,128)}) %reduce-scatter.5.cloned.1.call-update) | async-done | bytes 1572880 | tf_op jit(solution)/shard_map/reduce_scatter | solution.py:39
  (187 shorter events, 69.6 us)
Async XLA Ops:
  10.5 62.6 %copy-start.16 = (f32[8]{0:T(128)}, f32[8]{0:T(128)S(1)}, u32[]{:S(2)}) copy-start(f32[8]{0:T(128)S(1)} %fusion.97) | copy-start | bytes 100
  12.2 3.7 collective-permute-start.1
  13.5 6.5 %collective-permute-start = (f32[1,1,1,128,128]{4,3,2,1,0:T(8,128)S(1)}, f32[1,1,1,128,128]{4,3,2,1,0:T(8,128)S(1)}, u32[]{:S(2)}, u32[]{:S(2)}) collective-permute-start(f32[1,1,1,128,128]{4,3,2,1,0:T(8,128)S(1)} %slice.205), channel_id=1, source_target_pairs={{1,0},{2,1},{3,2},{4,3},{5,4},{6,5},{7,6},{8,7},{9,8},{10,9},{11,1... | collective-permute-start | bytes 196616 | tf_op jit(solution)/shard_map/ppermute | solution.py:22
  15.2 57.9 %copy-start.13 = (f32[3]{0:T(128)}, f32[3]{0:T(128)S(1)}, u32[]{:S(2)}) copy-start(f32[3]{0:T(128)S(1)} %get-tuple-element.327) | copy-start | bytes 40
  15.2 57.9 %copy-start.14 = (f32[3]{0:T(128)}, f32[3]{0:T(128)S(1)}, u32[]{:S(2)}) copy-start(f32[3]{0:T(128)S(1)} %get-tuple-element.328) | copy-start | bytes 40
  15.2 57.9 %copy-start.15 = (f32[3]{0:T(128)}, f32[3]{0:T(128)S(1)}, u32[]{:S(2)}) copy-start(f32[3]{0:T(128)S(1)} %get-tuple-element.329) | copy-start | bytes 40
  15.9 17.5 %copy-start.18 = (pred[8]{0:T(512)(128)(4,1)}, pred[8]{0:T(512)(128)(4,1)S(1)}, u32[]{:S(2)}) copy-start(pred[8]{0:T(512)(128)(4,1)S(1)} %iota_compare_fusion) | copy-start | bytes 28
  20.3 13.0 %copy-start.2 = (f32[8,128,128]{2,1,0:T(8,128)}, f32[8,128,128]{2,1,0:T(8,128)S(1)}, u32[]{:S(2)}) copy-start(f32[8,128,128]{2,1,0:T(8,128)S(1)} %get-tuple-element.371) | copy-start | bytes 1572868
  20.4 13.0 %copy-start.3 = (f32[8,128,128]{2,1,0:T(8,128)}, f32[8,128,128]{2,1,0:T(8,128)S(1)}, u32[]{:S(2)}) copy-start(f32[8,128,128]{2,1,0:T(8,128)S(1)} %get-tuple-element.373) | copy-start | bytes 1572868
  21.2 12.2 %copy-start.4 = (f32[8,128,128]{2,1,0:T(8,128)}, f32[8,128,128]{2,1,0:T(8,128)S(1)}, u32[]{:S(2)}) copy-start(f32[8,128,128]{2,1,0:T(8,128)S(1)} %get-tuple-element.385) | copy-start | bytes 1572868
  21.2 12.2 %copy-start.5 = (f32[8,128,128]{2,1,0:T(8,128)}, f32[8,128,128]{2,1,0:T(8,128)S(1)}, u32[]{:S(2)}) copy-start(f32[8,128,128]{2,1,0:T(8,128)S(1)} %get-tuple-element.386) | copy-start | bytes 1572868
  21.2 12.2 %copy-start.6 = (f32[8,128,128]{2,1,0:T(8,128)}, f32[8,128,128]{2,1,0:T(8,128)S(1)}, u32[]{:S(2)}) copy-start(f32[8,128,128]{2,1,0:T(8,128)S(1)} %get-tuple-element.391) | copy-start | bytes 1572868
  24.0 8.7 %collective-permute-start.2 = (f32[1,3,1,128,128]{4,3,2,1,0:T(8,128)S(1)}, f32[1,3,1,128,128]{4,3,2,1,0:T(8,128)S(1)}, u32[]{:S(2)}, u32[]{:S(2)}) collective-permute-start(f32[1,3,1,128,128]{4,3,2,1,0:T(8,128)S(1)} %slice.208), channel_id=1, source_target_pairs={{1,0},{2,1},{3,2},{4,3},{5,4},{6,5},{7,6},{8,7},{9,8},{10,9},{11,1... | collective-permute-start | bytes 589832 | tf_op jit(solution)/shard_map/ppermute | solution.py:22
  25.3 8.0 %collective-permute-start.3 = (f32[1,3,1,128,128]{4,3,2,1,0:T(8,128)S(1)}, f32[1,3,1,128,128]{4,3,2,1,0:T(8,128)S(1)}, u32[]{:S(2)}, u32[]{:S(2)}) collective-permute-start(f32[1,3,1,128,128]{4,3,2,1,0:T(8,128)S(1)} %bitcast.155), channel_id=1, source_target_pairs={{0,1},{1,2},{2,3},{3,4},{4,5},{5,6},{6,7},{7,8},{8,9},{9,10},{10,1... | collective-permute-start | bytes 589832 | tf_op jit(solution)/shard_map/ppermute | solution.py:21
  60.4 10.9 %all-to-all-start.1 = ((f32[16,1,1]{2,1,0:T(1,128)}), f32[16,1,1]{2,1,0:T(1,128)S(1)}, u32[]{:S(2)}, u32[]{:S(2)}) async-start(f32[16,1,1]{2,1,0:T(1,128)} %broadcast_in_dim.205), calls=%async_computation.1 | async-start | bytes 16384 | tf_op jit(solution)/shard_map/all_to_all | solution.py:29
  80.0 11.0 %all-to-all-start.2 = ((f32[16,1,1]{2,1,0:T(1,128)}), f32[16,1,1]{2,1,0:T(1,128)S(1)}, u32[]{:S(2)}, u32[]{:S(2)}) async-start(f32[16,1,1]{2,1,0:T(1,128)} %broadcast_in_dim.206), calls=%async_computation.2 | async-start | bytes 16384 | tf_op jit(solution)/shard_map/all_to_all | solution.py:29
  83.4 10.7 %collective-permute-start.4 = (f32[1,3,1,128,128]{4,3,2,1,0:T(8,128)S(1)}, f32[1,3,1,128,128]{4,3,2,1,0:T(8,128)}, u32[]{:S(2)}, u32[]{:S(2)}) collective-permute-start(f32[1,3,1,128,128]{4,3,2,1,0:T(8,128)S(1)} %slice.211), channel_id=1, source_target_pairs={{1,0},{2,1},{3,2},{4,3},{5,4},{6,5},{7,6},{8,7},{9,8},{10,9},{11,1... | collective-permute-start | bytes 589832 | tf_op jit(solution)/shard_map/ppermute | solution.py:22
  84.7 9.4 %collective-permute-start.5 = (f32[1,3,1,128,128]{4,3,2,1,0:T(8,128)S(1)}, f32[1,3,1,128,128]{4,3,2,1,0:T(8,128)}, u32[]{:S(2)}, u32[]{:S(2)}) collective-permute-start(f32[1,3,1,128,128]{4,3,2,1,0:T(8,128)S(1)} %bitcast.153), channel_id=1, source_target_pairs={{0,1},{1,2},{2,3},{3,4},{4,5},{5,6},{6,7},{7,8},{8,9},{9,10},{10,1... | collective-permute-start | bytes 589832 | tf_op jit(solution)/shard_map/ppermute | solution.py:21
  94.2 24.4 %copy-start.17 = (f32[8]{0:T(128)S(1)}, f32[8]{0:T(128)}, u32[]{:S(2)}) copy-start(f32[8]{0:T(128)} %copy-done.16) | copy-start | bytes 100
  100.2 16.4 %all-to-all-start.3 = ((f32[16,1,1]{2,1,0:T(1,128)}), f32[16,1,1]{2,1,0:T(1,128)S(1)}, u32[]{:S(2)}, u32[]{:S(2)}) async-start(f32[16,1,1]{2,1,0:T(1,128)} %broadcast_in_dim.209), calls=%async_computation.3 | async-start | bytes 16384 | tf_op jit(solution)/shard_map/all_to_all | solution.py:29
  109.2 262.0 %reduce-scatter.3.cloned.1.call-start = ((), (), s32[]{:S(2)}) async-start(), calls=%async_computation.6 | async-start | bytes 15728640 | tf_op jit(solution)/shard_map/reduce_scatter | solution.py:39
  120.2 4.6 %collective-permute-start.7 = (f32[1,3,1,128,128]{4,3,2,1,0:T(8,128)S(1)}, f32[1,3,1,128,128]{4,3,2,1,0:T(8,128)S(1)}, u32[]{:S(2)}, u32[]{:S(2)}) collective-permute-start(f32[1,3,1,128,128]{4,3,2,1,0:T(8,128)S(1)} %slice.214), channel_id=1, source_target_pairs={{1,0},{2,1},{3,2},{4,3},{5,4},{6,5},{7,6},{8,7},{9,8},{10,9},{11,1... | collective-permute-start | bytes 589832 | tf_op jit(solution)/shard_map/ppermute | solution.py:22
  121.5 4.1 collective-permute-start.6
  251.4 167.8 %reduce-scatter.5.cloned.1.call-start = ((), (), s32[]{:S(2)}) async-start(), calls=%async_computation.7 | async-start | bytes 4718592 | tf_op jit(solution)/shard_map/reduce_scatter | solution.py:39
  (10 other events, 33.6 us)
Sparse Core Ops, SparseCore 0:
  251.5 119.6 reduce-scatter.2
  373.5 45.6 reduce-scatter.4
where the time goes:
time: 428 us; the launch traced here: 426 us
  waiting for transfers between devices  188 us (44%)
  loops' own time  57.2 us (13%)
  matrix products  49.3 us (12%)
  starting transfers between devices  36.3 us (8%)
  local copies, waits for them, and re-layouts  27.3 us (6%)
  other arithmetic  24.8 us (6%)
  between operations  22.4 us (5%)
  blocking collectives  21.1 us (5%)
    reduce_scatter x2, waiting for transfers between devices, own_rows(): subtotal = lax.psum_scatter(subtotal, axis, scatter_dimension=0, tiled=True)  168 us
    another operation x1, loops' own time, per_device(): lax.map(one_target, jnp.arange(own_count * lax.axis_size(GRP), dtype=jnp....  57.2 us
    dot_general x8, matrix products, contribute(): jnp.einsum('pkn,pcnyx->pckyx', weight_z, pieces, precision=exact_mode)  28 us
    dot_general x8, matrix products, contribute(): jnp.einsum('pckyx,pmx->ckym', vertical, weight_x, precision=exact_mode)  21.3 us
    all_to_all x1, blocking collectives, copy_for_each(): return lax.all_to_all(copies, axis, split_axis=0, concat_axis=0, tiled=True)  21.1 us
    all_to_all x3, starting transfers between devices, copy_for_each(): return lax.all_to_all(copies, axis, split_axis=0, concat_axis=0, tiled=True)  15.8 us
    ppermute x4, starting transfers between devices, padded_2(): before = lax.ppermute(last, axis, up)  15.2 us
    all_to_all x3, waiting for transfers between devices, copy_for_each(): return lax.all_to_all(copies, axis, split_axis=0, concat_axis=0, tiled=True)  14.3 us
  transfers between devices with their start and end apart: 13, of which 8 were waited for; matrix products, arithmetic and copies ran while one was open for 1% of the time, Pallas kernels for 0%

commit v1 on v0

v1 whole, which is shorter than its diff:
```python
import functools
import jax
import jax.numpy as jnp
from jax import lax
from jax.experimental import pallas as pl
from jax.experimental.pallas import tpu as pltpu
from jax.sharding import PartitionSpec as P

MESH = pl.DeviceIdType.MESH
N_GRP = 8
N_Y = 4
OFFSETS = ((1, 0), (3, 0), (0, 1), (2, 0), (1, 1), (3, 1), (2, 1))
ROWS_UP = (1, 3, 7)


def peer_of(g, dy, dx):
    y, x = g // 2, g % 2
    return ((y + dy) % N_Y) * 2 + (x + dx) % 2


def fold8(v):
    total = v[0:8]
    for i in range(1, v.shape[0] // 8):
        total = total + v[8 * i : 8 * i + 8]
    return total


def body(
    n_s, f_hbm, k_hbm, aniso, coup, levels, neigh, out_hbm,
    f, kk, kz, gx, gy, fz, rj, z0, w, q1, kzup, kza, kzb, up, za, zb, qup, qa, qb,
    pz, pq, rz, rq, ru, corr, rc, ob, acc, mom, momr, tots, tot, cof,
    in_sem, out_sem, ks, kr, zs, zr, qs, qr, ms, mr, ts, tr, pzs, pzr, pqs, pqr, cs, cr,
):
    g = lax.axis_index("grp")
    s = lax.axis_index("slab")
    height, width = f.shape[2], f.shape[3]
    chunk = height // N_GRP
    below_id = (s + n_s - 1) % n_s
    above_id = (s + 1) % n_s

    barrier = pltpu.get_barrier_semaphore()
    for o in range(1, n_s):
        pl.semaphore_signal(barrier, inc=1, device_id={"slab": (s + o) % n_s}, device_id_type=MESH)
    for dy, dx in OFFSETS:
        pl.semaphore_signal(barrier, inc=1, device_id={"grp": peer_of(g, dy, dx)}, device_id_type=MESH)
    load_k = pltpu.make_async_copy(k_hbm.at[0], kk, in_sem.at[0])
    load_f = pltpu.make_async_copy(f_hbm.at[0], f, in_sem.at[1])
    load_k.start()
    load_f.start()

    def sizes(lx, lz):
        nx = jnp.where(lx == 2, width, jnp.where(lx == 1, width // 2, width // 4))
        a = jnp.where(lz == 2, 8, jnp.where(lz == 1, 4, 2))
        return nx, a

    nx, a = sizes(levels[g, 0], levels[g, 1])
    sx = nx.astype(jnp.float32) * (1.0 / height)
    sz = (a * n_s).astype(jnp.float32) * (1.0 / height)
    scale = (sx * sx, 1.0, sz * sz)
    cf = [[aniso[0, c, d] * scale[d] for d in range(3)] for c in range(3)]
    cp = [[coup[0, c, e] for e in range(3)] for c in range(3)]
    sel = [(a == j + 1).astype(jnp.float32) for j in ROWS_UP]
    has_below = (s > 0).astype(jnp.float32)
    has_above = (s < n_s - 1).astype(jnp.float32)

    lane = lax.broadcasted_iota(jnp.int32, (height, width), 1)
    row = lax.broadcasted_iota(jnp.int32, (height, width), 0)
    lane_on = (lane < nx).astype(jnp.float32)

    def top_row(read):
        return sel[0] * read(1) + sel[1] * read(3) + sel[2] * read(7)

    def remote(src, dst, ssem, rsem, device_id):
        return pltpu.make_async_remote_copy(
            src_ref=src, dst_ref=dst, send_sem=ssem, recv_sem=rsem,
            device_id=device_id, device_id_type=MESH,
        )

    def halo(down_src, up_src, above_dst, below_dst, ssem, rsem):
        return (
            remote(down_src, above_dst, ssem.at[0], rsem.at[0], {"slab": below_id}),
            remote(up_src, below_dst, ssem.at[1], rsem.at[1], {"slab": above_id}),
        )

    load_k.wait()
    kzup[...] = top_row(lambda j: kk[2, j])
    pl.semaphore_wait(barrier, n_s - 1 + len(OFFSETS))
    k_halo = halo(kk.at[2, 0], kzup, kza, kzb, ks, kr)
    for cpy in k_halo:
        cpy.start()
    load_f.wait()

    zero = jnp.zeros((height, width), jnp.float32)
    for buf in (z0, q1):
        for c in range(3):
            buf[c, 0] = zero
            buf[c, 9] = zero
    kz[8] = zero
    acc[...] = jnp.zeros_like(acc)

    def faces(k, carry):
        on = lane_on * (k < a).astype(jnp.float32)
        kx = kk[0, k] * on
        ky = kk[1, k] * on
        kz[k] = kk[2, k] * on
        x_up = pltpu.roll(kx, width - 1, 1)
        x_up = jnp.where(lane < width - 1, x_up, 0.0)
        x_down = jnp.where(lane > 0, pltpu.roll(kx, 1, 1), 0.0)
        gx[k] = jnp.where(lane < nx - 1, 0.5 * (kx + x_up), 0.0)
        y_up = jnp.where(row < height - 1, pltpu.roll(ky, height - 1, 0), 0.0)
        y_down = jnp.where(row > 0, pltpu.roll(ky, 1, 0), 0.0)
        gy[k] = jnp.where(row < height - 1, 0.5 * (ky + y_up), 0.0)
        sum_x = kx + 0.5 * (x_up + x_down)
        sum_y = ky + 0.5 * (y_up + y_down)
        for c in range(3):
            rj[c, k] = cp[c][c] + cf[c][0] * sum_x + cf[c][1] * sum_y
            f[c, k] = f[c, k] * on
        return carry

    lax.fori_loop(0, 8, faces, 0)

    for cpy in k_halo:
        cpy.wait()
    fz[0] = 0.5 * (kzb[...] * (lane_on * has_below) + kz[0])
    rim_k = kza[...] * (lane_on * has_above)

    def z_faces(j, carry):
        top = (j == a).astype(jnp.float32)
        fz[j] = 0.5 * (kz[j - 1] + kz[j] + top * rim_k)
        return carry

    lax.fori_loop(1, 9, z_faces, 0)

    def first(k, carry):
        sum_z = fz[k] + fz[k + 1]
        for c in range(3):
            inverse = 1.0 / (rj[c, k] + cf[c][2] * sum_z)
            rj[c, k] = inverse
            fc = f[c, k]
            zc = fc * inverse
            z0[c, k + 1] = zc
            acc[0] += fold8(fc * zc)
        return carry

    lax.fori_loop(0, 8, first, 0)
    for c in range(3):
        up[c] = top_row(lambda j: z0[c, j + 1])
    z_halo = halo(z0.at[:, 1], up, za, zb, zs, zr)
    for cpy in z_halo:
        cpy.start()

    def apply_row(u, base, c, k, values):
        uc = values[c]
        out = base
        for e in range(3):
            if e != c:
                out = out + cp[c][e] * values[e]
        gxk = gx[k]
        gyk = gy[k]
        nb_x = gxk * pltpu.roll(uc, width - 1, 1) + pltpu.roll(gxk * uc, 1, 1)
        nb_y = gyk * pltpu.roll(uc, height - 1, 0) + pltpu.roll(gyk * uc, 1, 0)
        inside = (k < a).astype(jnp.float32)
        nb_z = fz[k + 1] * u[c, k + 2] + (inside * fz[k]) * u[c, k]
        return out - (cf[c][0] * nb_x + cf[c][1] * nb_y + cf[c][2] * nb_z)

    def second(k, carry):
        values = [z0[c, k + 1] for c in range(3)]
        for c in range(3):
            w[c, k] = apply_row(z0, f[c, k], c, k, values)
        return carry

    lax.fori_loop(0, 8, second, 0)
    for cpy in z_halo:
        cpy.wait()
    for c in range(3):
        zb[c] = zb[c] * has_below
        za[c] = za[c] * has_above
        w[c, 0] -= cf[c][2] * (fz[0] * zb[c])
        for i, j in enumerate(ROWS_UP):
            w[c, j] -= (sel[i] * cf[c][2]) * (fz[j + 1] * za[c])

    def third(k, carry):
        for c in range(3):
            wc = w[c, k]
            qc = wc * rj[c, k]
            q1[c, k + 1] = qc
            acc[1] += fold8(z0[c, k + 1] * wc)
            acc[2] += fold8(wc * qc)
        return carry

    lax.fori_loop(0, 8, third, 0)
    for c in range(3):
        qup[c] = top_row(lambda j: q1[c, j + 1])
    q_halo = halo(q1.at[:, 1], qup, qa, qb, qs, qr)
    for cpy in q_halo:
        cpy.start()

    full = (a == 8).astype(jnp.float32)
    part = 1.0 - full

    def pack(u, ua, ub, dst):
        def one(c, carry):
            for r in range(6):
                if r == 0:
                    loose = ub[c]
                elif r == 3:
                    loose = u[c, 3] + sel[0] * ua[c]
                elif r == 5:
                    loose = sel[1] * ua[c]
                else:
                    loose = u[c, r]
                value = part * loose
                if r < 4:
                    value = value + full * (u[c, r + 1] + pltpu.roll(u[c, r + 5], width // 2, 1))
                dst[c, r] = value
            return carry

        lax.fori_loop(0, 3, one, 0)

    def rows_of(i):
        return pl.ds(pl.multiple_of(i * chunk, chunk), chunk)

    def scatter(src, dst, ssem, rsem):
        copies = []
        for o, (dy, dx) in enumerate(OFFSETS):
            to = peer_of(g, dy, dx)
            copies.append(
                remote(src.at[:, :, rows_of(to)], dst.at[g], ssem.at[o], rsem.at[o], {"grp": to})
            )
        return copies

    def await_from(dst, ssem, rsem, o):
        dy, dx = OFFSETS[o]
        source = peer_of(g, N_Y - dy, dx)
        remote(dst.at[source], dst.at[source], ssem.at[o], rsem.at[o], {"grp": source}).wait_recv()

    pack(z0, za, zb, pz)
    z_out = scatter(pz, rz, pzs, pzr)
    for cpy in z_out:
        cpy.start()

    def fourth(k, carry):
        values = [q1[c, k + 1] for c in range(3)]
        for c in range(3):
            acc[3] += fold8(values[c] * apply_row(q1, w[c, k], c, k, values))
        return carry

    lax.fori_loop(0, 8, fourth, 0)
    for cpy in q_halo:
        cpy.wait()
    for c in range(3):
        qb[c] = qb[c] * has_below
        qa[c] = qa[c] * has_above
        cross = q1[c, 1] * (fz[0] * qb[c])
        for i, j in enumerate(ROWS_UP):
            cross = cross + sel[i] * (q1[c, j + 1] * (fz[j + 1] * qa[c]))
        acc[3] -= cf[c][2] * fold8(cross)

    for i in range(4):
        mom[i : i + 1] = jnp.sum(acc[i], axis=0, keepdims=True)
    mom[4:8] = jnp.zeros((4, width), jnp.float32)
    m_out = []
    for o in range(1, n_s):
        to = (s + o) % n_s
        m_out.append(remote(mom, momr.at[s], ms.at[o - 1], mr.at[o - 1], {"slab": to}))
    for cpy in m_out:
        cpy.start()

    pack(q1, qa, qb, pq)
    q_out = scatter(pq, rq, pqs, pqr)
    for cpy in q_out:
        cpy.start()
    momr[s] = mom[...]
    rz[g] = pz[:, :, rows_of(g)]
    rq[g] = pq[:, :, rows_of(g)]

    for o in range(1, n_s):
        source = (s + n_s - o) % n_s
        remote(
            momr.at[source], momr.at[source], ms.at[o - 1], mr.at[o - 1], {"slab": source}
        ).wait_recv()
    total = momr[0]
    for i in range(1, n_s):
        total = total + momr[i]
    tots[...] = total
    t_out = []
    for o, (dy, dx) in enumerate(OFFSETS):
        to = peer_of(g, dy, dx)
        t_out.append(remote(tots, tot.at[g], ts.at[o], tr.at[o], {"grp": to}))
    for cpy in t_out:
        cpy.start()
    tot[g] = tots[...]
    for o in range(len(OFFSETS)):
        await_from(tot, ts, tr, o)
    sums = jnp.sum(tot[...], axis=2, keepdims=True)
    rz0, m1, m2, m3 = (sums[:, i : i + 1] for i in range(4))
    step0 = rz0 / m1
    rz1 = step0 * step0 * m2 - rz0
    beta = rz1 / rz0
    bend = m1 - 2.0 * step0 * m2 + step0 * step0 * m3
    step1 = jnp.clip(rz1 / (bend - beta * rz1 / step0), 0.25, 1024.0)
    cof[0] = jnp.broadcast_to(step0 + step1 * (1.0 + beta), (N_GRP, 8, width))
    cof[1] = jnp.broadcast_to(-step1 * step0, (N_GRP, 8, width))

    for o in range(len(OFFSETS)):
        await_from(rz, pzs, pzr, o)
    for o in range(len(OFFSETS)):
        await_from(rq, pqs, pqr, o)

    def combine(p, carry):
        c0 = jnp.broadcast_to(cof[0, p][0:1], (chunk, width))
        c1 = jnp.broadcast_to(cof[1, p][0:1], (chunk, width))
        for c in range(3):
            for r in range(6):
                ru[p, c, r] = c0 * rz[p, c, r] + c1 * rq[p, c, r]
        return carry

    lax.fori_loop(0, N_GRP, combine, 0)

    lanes = lax.broadcasted_iota(jnp.int32, (chunk, width), 1)
    half = lanes // 2
    beside = jnp.where(lanes % 2 == 1, half + 1, half + (width - 1)) % width
    low = (lanes < width // 2).astype(jnp.float32)

    def mix(t):
        lx, lz = levels[t, 0], levels[t, 1]
        nx_t, a_t = sizes(lx, lz)
        ids = [neigh[t, i] for i in range(3)]
        there = [(i >= 0).astype(jnp.float32) for i in ids]
        n0, n1, n2 = (jnp.maximum(i, 0) for i in ids)
        full_t = (a_t == 8).astype(jnp.float32)
        near = full_t * there[0]
        far = (1.0 - full_t) * there[0]
        on_x = (lanes < nx_t).astype(jnp.float32)

        def one(c, carry):
            for k in range(8):
                m = k // 2
                other = m + 2 * (k % 2)
                if k < 4:
                    v = near * ru[n0, c, k] + far * ru[n0, c, k + 1]
                else:
                    v = near * pltpu.roll(ru[n0, c, k - 4], width // 2, 1)
                v = v * low
                v = v - there[2] * (0.75 * ru[n2, c, m + 1] + 0.25 * ru[n2, c, other])
                x = 0.75 * jnp.take_along_axis(v, half, axis=1) + 0.25 * jnp.take_along_axis(
                    v, beside, axis=1
                )
                x = x + there[1] * (0.75 * ru[n1, c, m + 1] + 0.25 * ru[n1, c, other])
                corr[t, c, k] = x * (on_x * (k < a_t).astype(jnp.float32))
            return carry

        lax.fori_loop(0, 3, one, 0)

    c_out = []
    for o, (dy, dx) in enumerate(OFFSETS):
        to = peer_of(g, dy, dx)
        mix(to)
        cpy = remote(corr.at[to], rc.at[g], cs.at[o], cr.at[o], {"grp": to})
        cpy.start()
        c_out.append(cpy)
    mix(g)
    own0 = jnp.broadcast_to(cof[0, g][0:1], (height, width))
    own1 = jnp.broadcast_to(cof[1, g][0:1], (height, width))

    def own(k, carry):
        for c in range(3):
            ob[c, k] = own0 * z0[c, k + 1] + own1 * q1[c, k + 1]
        return carry

    lax.fori_loop(0, 8, own, 0)

    def finish(source, ref, i):
        rows = rows_of(source)

        def one(k, carry):
            for c in range(3):
                ob[c, k, rows] = ob[c, k, rows] - ref[source, c, k]
            return carry

        lax.fori_loop(0, 8, one, 0)
        cpy = pltpu.make_async_copy(ob.at[:, :, rows], out_hbm.at[0, :, :, rows], out_sem.at[i])
        cpy.start()
        return cpy

    outs = [finish(g, corr, 0)]
    for o, (dy, dx) in enumerate(OFFSETS):
        await_from(rc, cs, cr, o)
        outs.append(finish(peer_of(g, N_Y - dy, dx), rc, o + 1))
    for cpy in z_out + q_out + m_out + t_out + c_out:
        cpy.wait_send()
    for cpy in outs:
        cpy.wait()


def solution(mesh):
    n_s = mesh.shape["slab"]

    def per_device(forcing, stiffness, anisotropy, coupling, levels, neighbours):
        _, _, depth, height, width = forcing.shape
        chunk = height // N_GRP
        plane = (height, width)
        f32 = jnp.float32
        dma = pltpu.SemaphoreType.DMA
        anyspec = pl.BlockSpec(memory_space=pl.ANY)
        smem = pl.BlockSpec(memory_space=pltpu.SMEM)
        vm = lambda *shape: pltpu.VMEM(shape, f32)
        others = len(OFFSETS)
        scratch = [
            vm(3, 8, *plane), vm(3, 8, *plane), vm(9, *plane), vm(8, *plane), vm(8, *plane),
            vm(9, *plane), vm(3, 8, *plane), vm(3, 10, *plane), vm(3, 8, *plane),
            vm(3, 10, *plane),
            vm(*plane), vm(*plane), vm(*plane),
            vm(3, *plane), vm(3, *plane), vm(3, *plane),
            vm(3, *plane), vm(3, *plane), vm(3, *plane),
            vm(3, 6, *plane), vm(3, 6, *plane),
            vm(N_GRP, 3, 6, chunk, width), vm(N_GRP, 3, 6, chunk, width),
            vm(N_GRP, 3, 6, chunk, width),
            vm(N_GRP, 3, 8, chunk, width), vm(N_GRP, 3, 8, chunk, width),
            vm(3, 8, *plane),
            vm(4, 8, width), vm(8, width), vm(n_s, 8, width), vm(8, width),
            vm(N_GRP, 8, width), vm(2, N_GRP, 8, width),
            dma((2,)), dma((N_GRP,)),
            dma((2,)), dma((2,)), dma((2,)), dma((2,)), dma((2,)), dma((2,)),
            dma((n_s - 1,)), dma((n_s - 1,)),
            dma((others,)), dma((others,)), dma((others,)), dma((others,)),
            dma((others,)), dma((others,)), dma((others,)), dma((others,)),
        ]
        return pl.pallas_call(
            functools.partial(body, n_s),
            out_shape=jax.ShapeDtypeStruct(forcing.shape, f32),
            in_specs=[anyspec, anyspec, smem, smem, smem, smem],
            out_specs=anyspec,
            scratch_shapes=scratch,
            compiler_params=pltpu.CompilerParams(
                collective_id=0, has_side_effects=True, vmem_limit_bytes=56 * 1024 * 1024
            ),
        )(forcing, stiffness, anisotropy, coupling, levels, neighbours)

    wide = P("grp", None, "slab", None, None)
    small = P("grp", None, None)
    return jax.shard_map(
        per_device,
        mesh=mesh,
        in_specs=(wide, wide, small, small, P(), P()),
        out_specs=wide,
        check_vma=False,
    )
```

time: 428 us -> 85.5 us (0.20)
  waiting for transfers between devices: 188 us -> 0 us
  Pallas kernels: 0 us -> 77.3 us
  loops' own time: 57.2 us -> 0 us
  matrix products: 49.3 us -> 0 us
  starting transfers between devices: 36.3 us -> 0 us
  other arithmetic: 24.8 us -> 0 us
  between operations: 22.4 us -> 0.01 us
  blocking collectives: 21.1 us -> 0 us
  local copies, waits for them, and re-layouts: 27.3 us -> 7.89 us
    reduce_scatter x2 -> x0, waiting for transfers between devices: 168 us -> none  [own_rows(): subtotal = lax.psum_scatter(subtotal, axis, scatter_dimension=0, tiled=True)]
    pallas_call x0 -> x1, Pallas kernels: none -> 77.3 us  [per_device(): pl.pallas_call(functools.partial(body, n_s), out_shape=jax.ShapeDtypeStru...]
    another operation x1 -> x0, loops' own time: 57.2 us -> none  [per_device(): lax.map(one_target, jnp.arange(own_count * lax.axis_size(GRP), dtype=jnp....]
    dot_general x16 -> x0, matrix products: 49.3 us -> none  [the longest x8 28 us: contribute(): jnp.einsum('pkn,pcnyx->pckyx', weight_z, pieces, precision=exact_mode)]
    all_to_all x1 -> x0, blocking collectives: 21.1 us -> none  [copy_for_each(): return lax.all_to_all(copies, axis, split_axis=0, concat_axis=0, tiled=True)]
    ppermute x8 -> x0, starting transfers between devices: 20.4 us -> none  [the longest x4 15.2 us: padded_2(): before = lax.ppermute(last, axis, up)]
    reduce_sum x12 -> x0, other arithmetic: 18.3 us -> none  [the longest x2 8.86 us: pair_sums(): return jnp.sum(first * second, axis=(1, 2, 3, 4))]
    all_to_all x3 -> x0, starting transfers between devices: 15.8 us -> none  [copy_for_each(): return lax.all_to_all(copies, axis, split_axis=0, concat_axis=0, tiled=True)]
  transfers between devices with their start and end apart: 13 -> 0, of which waited for: 8 -> 0; matrix products, arithmetic and copies ran while one was open for 1% -> 0% of each run, Pallas kernels for 0% -> 0%
where the time goes in v1:
time: 85.5 us; the launch traced here: 85.2 us
  Pallas kernels  77.3 us (90%)
  local copies, waits for them, and re-layouts  7.89 us (9%)
    pallas_call x1, Pallas kernels, per_device(): pl.pallas_call(functools.partial(body, n_s), out_shape=jax.ShapeDtypeStru...  77.3 us
    unnamed x5, local copies, waits for them, and re-layouts  7.89 us

profile of v1, /device:TPU:0, one launch (start us, length us, event | category | flops | bytes accessed | tf_op | source)
XLA Modules:
  0.0 85.2 jit_solution(2112393064625498665)
XLA Ops:
  0.0 1.3 %copy.7.aniso = f32[1,3,3]{2,1,0:T(4,128)} copy(f32[1,3,3]{2,0,1:T(1,128)} %param.8) | data formatting | bytes 72 | tf_op args[2]
  1.3 1.2 %copy.8.coup = f32[1,3,3]{2,1,0:T(4,128)} copy(f32[1,3,3]{2,0,1:T(1,128)} %param.9) | data formatting | bytes 72 | tf_op args[3]
  2.5 1.3 %copy.9.levels = s32[8,2]{1,0:T(8,128)} copy(s32[8,2]{0,1:T(2,128)} %param.10) | data formatting | bytes 128 | tf_op args[4]
  3.8 1.3 %copy.10.neigh = s32[8,3]{1,0:T(8,128)} copy(s32[8,3]{0,1:T(4,128)} %param.11) | data formatting | bytes 192 | tf_op args[5]
  5.2 77.3 %shard_map.64 = f32[1,3,8,128,128]{4,3,2,1,0:T(8,128)} custom-call(f32[1,3,8,128,128]{4,3,2,1,0:T(8,128)} %f_hbm.1, f32[1,3,8,128,128]{4,3,2,1,0:T(8,128)} %k_hbm.1, f32[1,3,3]{2,1,0:T(4,128)} %copy.7.aniso, f32[1,3,3]{2,1,0:T(4,128)} %copy.8.coup, s32[8,2]{1,0:T(8,128)} %copy.9.levels, s32[8,3]{1,0:T(8,128)} %copy.10.neigh), custom_call_target="tpu_custom_call" | custom-call | tf_op jit(solution)/shard_map/pallas_call | solution.py:429
  82.5 2.7 %copy.12 = f32[1,3,8,128,128]{4,3,2,1,0:T(8,128)} copy(f32[1,3,8,128,128]{4,3,2,1,0:T(8,128)} %shard_map.64) | data formatting | bytes 3145728

commit v2 on v1

--- a/solution.py
+++ b/solution.py
@@ -26,10 +26,11 @@
 
 
 def body(
-    n_s, f_hbm, k_hbm, aniso, coup, levels, neigh, out_hbm,
+    n_s, f_hbm, k_hbm, aniso_hbm, coup_hbm, levels_hbm, neigh_hbm, out,
+    aniso, coup, levels, neigh,
     f, kk, kz, gx, gy, fz, rj, z0, w, q1, kzup, kza, kzb, up, za, zb, qup, qa, qb,
-    pz, pq, rz, rq, ru, corr, rc, ob, acc, mom, momr, tots, tot, cof,
-    in_sem, out_sem, ks, kr, zs, zr, qs, qr, ms, mr, ts, tr, pzs, pzr, pqs, pqr, cs, cr,
+    pu, ru, corr, rc, acc, mom, momr,
+    in_sem, ks, kr, zs, zr, qs, qr, ms, mr, ps, pr, cs, cr,
 ):
     g = lax.axis_index("grp")
     s = lax.axis_index("slab")
@@ -45,20 +46,30 @@
         pl.semaphore_signal(barrier, inc=1, device_id={"grp": peer_of(g, dy, dx)}, device_id_type=MESH)
     load_k = pltpu.make_async_copy(k_hbm.at[0], kk, in_sem.at[0])
     load_f = pltpu.make_async_copy(f_hbm.at[0], f, in_sem.at[1])
+    smalls = [
+        pltpu.make_async_copy(src, dst, in_sem.at[2 + i])
+        for i, (src, dst) in enumerate(
+            ((levels_hbm, levels), (aniso_hbm, aniso), (coup_hbm, coup), (neigh_hbm, neigh))
+        )
+    ]
+    for cpy in smalls:
+        cpy.start()
     load_k.start()
     load_f.start()
+    for cpy in smalls:
+        cpy.wait()
 
     def sizes(lx, lz):
         nx = jnp.where(lx == 2, width, jnp.where(lx == 1, width // 2, width // 4))
         a = jnp.where(lz == 2, 8, jnp.where(lz == 1, 4, 2))
         return nx, a
 
-    nx, a = sizes(levels[g, 0], levels[g, 1])
+    nx, a = sizes(levels[0, g], levels[1, g])
     sx = nx.astype(jnp.float32) * (1.0 / height)
     sz = (a * n_s).astype(jnp.float32) * (1.0 / height)
     scale = (sx * sx, 1.0, sz * sz)
-    cf = [[aniso[0, c, d] * scale[d] for d in range(3)] for c in range(3)]
-    cp = [[coup[0, c, e] for e in range(3)] for c in range(3)]
+    cf = [[aniso[c, 0, d] * scale[d] for d in range(3)] for c in range(3)]
+    cp = [[coup[c, 0, e] for e in range(3)] for c in range(3)]
     sel = [(a == j + 1).astype(jnp.float32) for j in ROWS_UP]
     has_below = (s > 0).astype(jnp.float32)
     has_above = (s < n_s - 1).astype(jnp.float32)
@@ -198,25 +209,6 @@
     full = (a == 8).astype(jnp.float32)
     part = 1.0 - full
 
-    def pack(u, ua, ub, dst):
-        def one(c, carry):
-            for r in range(6):
-                if r == 0:
-                    loose = ub[c]
-                elif r == 3:
-                    loose = u[c, 3] + sel[0] * ua[c]
-                elif r == 5:
-                    loose = sel[1] * ua[c]
-                else:
-                    loose = u[c, r]
-                value = part * loose
-                if r < 4:
-                    value = value + full * (u[c, r + 1] + pltpu.roll(u[c, r + 5], width // 2, 1))
-                dst[c, r] = value
-            return carry
-
-        lax.fori_loop(0, 3, one, 0)
-
     def rows_of(i):
         return pl.ds(pl.multiple_of(i * chunk, chunk), chunk)
 
@@ -233,11 +225,6 @@
         dy, dx = OFFSETS[o]
         source = peer_of(g, N_Y - dy, dx)
         remote(dst.at[source], dst.at[source], ssem.at[o], rsem.at[o], {"grp": source}).wait_recv()
-
-    pack(z0, za, zb, pz)
-    z_out = scatter(pz, rz, pzs, pzr)
-    for cpy in z_out:
-        cpy.start()
 
     def fourth(k, carry):
         values = [q1[c, k + 1] for c in range(3)]
@@ -266,14 +253,7 @@
     for cpy in m_out:
         cpy.start()
 
-    pack(q1, qa, qb, pq)
-    q_out = scatter(pq, rq, pqs, pqr)
-    for cpy in q_out:
-        cpy.start()
     momr[s] = mom[...]
-    rz[g] = pz[:, :, rows_of(g)]
-    rq[g] = pq[:, :, rows_of(g)]
-
     for o in range(1, n_s):
         source = (s + n_s - o) % n_s
         remote(
@@ -282,40 +262,43 @@
     total = momr[0]
     for i in range(1, n_s):
         total = total + momr[i]
-    tots[...] = total
-    t_out = []
-    for o, (dy, dx) in enumerate(OFFSETS):
-        to = peer_of(g, dy, dx)
-        t_out.append(remote(tots, tot.at[g], ts.at[o], tr.at[o], {"grp": to}))
-    for cpy in t_out:
-        cpy.start()
-    tot[g] = tots[...]
-    for o in range(len(OFFSETS)):
-        await_from(tot, ts, tr, o)
-    sums = jnp.sum(tot[...], axis=2, keepdims=True)
-    rz0, m1, m2, m3 = (sums[:, i : i + 1] for i in range(4))
+    sums = jnp.sum(total, axis=1, keepdims=True)
+    rz0, m1, m2, m3 = (sums[i : i + 1] for i in range(4))
     step0 = rz0 / m1
     rz1 = step0 * step0 * m2 - rz0
     beta = rz1 / rz0
     bend = m1 - 2.0 * step0 * m2 + step0 * step0 * m3
     step1 = jnp.clip(rz1 / (bend - beta * rz1 / step0), 0.25, 1024.0)
-    cof[0] = jnp.broadcast_to(step0 + step1 * (1.0 + beta), (N_GRP, 8, width))
-    cof[1] = jnp.broadcast_to(-step1 * step0, (N_GRP, 8, width))
-
+    on_z = jnp.broadcast_to(step0 + step1 * (1.0 + beta), (height, width))
+    on_q = jnp.broadcast_to(-step1 * step0, (height, width))
+
+    def solve(c, carry):
+        rows = [on_z * z0[c, k + 1] + on_q * q1[c, k + 1] for k in range(8)]
+        rim_below = on_z * zb[c] + on_q * qb[c]
+        rim_above = on_z * za[c] + on_q * qa[c]
+        for k in range(8):
+            out[0, c, k] = rows[k]
+        for r in range(6):
+            if r == 0:
+                value = part * rim_below
+            elif r == 3:
+                value = part * (rows[2] + sel[0] * rim_above)
+            elif r == 5:
+                value = sel[1] * rim_above
+            else:
+                value = part * rows[r - 1]
+            if r < 4:
+                value = value + full * (rows[r] + pltpu.roll(rows[r + 4], width // 2, 1))
+            pu[c, r] = value
+        return carry
+
+    lax.fori_loop(0, 3, solve, 0)
+    p_out = scatter(pu, ru, ps, pr)
+    for cpy in p_out:
+        cpy.start()
+    ru[g] = pu[:, :, rows_of(g)]
     for o in range(len(OFFSETS)):
-        await_from(rz, pzs, pzr, o)
-    for o in range(len(OFFSETS)):
-        await_from(rq, pqs, pqr, o)
-
-    def combine(p, carry):
-        c0 = jnp.broadcast_to(cof[0, p][0:1], (chunk, width))
-        c1 = jnp.broadcast_to(cof[1, p][0:1], (chunk, width))
-        for c in range(3):
-            for r in range(6):
-                ru[p, c, r] = c0 * rz[p, c, r] + c1 * rq[p, c, r]
-        return carry
-
-    lax.fori_loop(0, N_GRP, combine, 0)
+        await_from(ru, ps, pr, o)
 
     lanes = lax.broadcasted_iota(jnp.int32, (chunk, width), 1)
     half = lanes // 2
@@ -323,9 +306,9 @@
     low = (lanes < width // 2).astype(jnp.float32)
 
     def mix(t):
-        lx, lz = levels[t, 0], levels[t, 1]
+        lx, lz = levels[0, t], levels[1, t]
         nx_t, a_t = sizes(lx, lz)
-        ids = [neigh[t, i] for i in range(3)]
+        ids = [neigh[i, t] for i in range(3)]
         there = [(i >= 0).astype(jnp.float32) for i in ids]
         n0, n1, n2 = (jnp.maximum(i, 0) for i in ids)
         full_t = (a_t == 8).astype(jnp.float32)
@@ -360,37 +343,23 @@
         cpy.start()
         c_out.append(cpy)
     mix(g)
-    own0 = jnp.broadcast_to(cof[0, g][0:1], (height, width))
-    own1 = jnp.broadcast_to(cof[1, g][0:1], (height, width))
-
-    def own(k, carry):
-        for c in range(3):
-            ob[c, k] = own0 * z0[c, k + 1] + own1 * q1[c, k + 1]
-        return carry
-
-    lax.fori_loop(0, 8, own, 0)
-
-    def finish(source, ref, i):
+
+    def finish(source, ref):
         rows = rows_of(source)
 
         def one(k, carry):
             for c in range(3):
-                ob[c, k, rows] = ob[c, k, rows] - ref[source, c, k]
+                out[0, c, k, rows] = out[0, c, k, rows] - ref[source, c, k]
             return carry
 
         lax.fori_loop(0, 8, one, 0)
-        cpy = pltpu.make_async_copy(ob.at[:, :, rows], out_hbm.at[0, :, :, rows], out_sem.at[i])
-        cpy.start()
-        return cpy
-
-    outs = [finish(g, corr, 0)]
+
+    finish(g, corr)
     for o, (dy, dx) in enumerate(OFFSETS):
         await_from(rc, cs, cr, o)
-        outs.append(finish(peer_of(g, N_Y - dy, dx), rc, o + 1))
-    for cpy in z_out + q_out + m_out + t_out + c_out:
+        finish(peer_of(g, N_Y - dy, dx), rc)
+    for cpy in m_out + p_out + c_out:
         cpy.wait_send()
-    for cpy in outs:
-        cpy.wait()
 
 
 def solution(mesh):
@@ -398,39 +367,39 @@
 
     def per_device(forcing, stiffness, anisotropy, coupling, levels, neighbours):
         _, _, depth, height, width = forcing.shape
+        anisotropy = jnp.transpose(anisotropy, (1, 0, 2))
+        coupling = jnp.transpose(coupling, (1, 0, 2))
+        levels = levels.T
+        neighbours = neighbours.T
         chunk = height // N_GRP
         plane = (height, width)
         f32 = jnp.float32
         dma = pltpu.SemaphoreType.DMA
         anyspec = pl.BlockSpec(memory_space=pl.ANY)
-        smem = pl.BlockSpec(memory_space=pltpu.SMEM)
         vm = lambda *shape: pltpu.VMEM(shape, f32)
         others = len(OFFSETS)
         scratch = [
+            pltpu.SMEM(anisotropy.shape, f32), pltpu.SMEM(coupling.shape, f32),
+            pltpu.SMEM(levels.shape, jnp.int32), pltpu.SMEM(neighbours.shape, jnp.int32),
             vm(3, 8, *plane), vm(3, 8, *plane), vm(9, *plane), vm(8, *plane), vm(8, *plane),
             vm(9, *plane), vm(3, 8, *plane), vm(3, 10, *plane), vm(3, 8, *plane),
             vm(3, 10, *plane),
             vm(*plane), vm(*plane), vm(*plane),
             vm(3, *plane), vm(3, *plane), vm(3, *plane),
             vm(3, *plane), vm(3, *plane), vm(3, *plane),
-            vm(3, 6, *plane), vm(3, 6, *plane),
-            vm(N_GRP, 3, 6, chunk, width), vm(N_GRP, 3, 6, chunk, width),
-            vm(N_GRP, 3, 6, chunk, width),
+            vm(3, 6, *plane), vm(N_GRP, 3, 6, chunk, width),
             vm(N_GRP, 3, 8, chunk, width), vm(N_GRP, 3, 8, chunk, width),
-            vm(3, 8, *plane),
-            vm(4, 8, width), vm(8, width), vm(n_s, 8, width), vm(8, width),
-            vm(N_GRP, 8, width), vm(2, N_GRP, 8, width),
-            dma((2,)), dma((N_GRP,)),
+            vm(4, 8, width), vm(8, width), vm(n_s, 8, width),
+            dma((6,)),
             dma((2,)), dma((2,)), dma((2,)), dma((2,)), dma((2,)), dma((2,)),
             dma((n_s - 1,)), dma((n_s - 1,)),
-            dma((others,)), dma((others,)), dma((others,)), dma((others,)),
             dma((others,)), dma((others,)), dma((others,)), dma((others,)),
         ]
         return pl.pallas_call(
             functools.partial(body, n_s),
-            out_shape=jax.ShapeDtypeStruct(forcing.shape, f32),
-            in_specs=[anyspec, anyspec, smem, smem, smem, smem],
-            out_specs=anyspec,
+            out_shape=pltpu.VMEM(forcing.shape, f32),
+            in_specs=[anyspec] * 6,
+            out_specs=pl.BlockSpec(memory_space=pltpu.VMEM),
             scratch_shapes=scratch,
             compiler_params=pltpu.CompilerParams(
                 collective_id=0, has_side_effects=True, vmem_limit_bytes=56 * 1024 * 1024

time: 85.5 us -> 70.5 us (0.82)
  Pallas kernels: 77.3 us -> 68.9 us
  local copies, waits for them, and re-layouts: 7.89 us -> 1.15 us
    pallas_call x1, Pallas kernels: 77.3 us -> 68.9 us  [per_device(): pl.pallas_call(functools.partial(body, n_s), out_shape=pltpu.VMEM(forcing...]
    unnamed x5 -> x1, local copies, waits for them, and re-layouts: 7.89 us -> 1.15 us
where the time goes in v2:
time: 70.5 us; the launch traced here: 70.1 us
  Pallas kernels  68.9 us (98%)
  local copies, waits for them, and re-layouts  1.15 us (2%)
    pallas_call x1, Pallas kernels, per_device(): pl.pallas_call(functools.partial(body, n_s), out_shape=pltpu.VMEM(forcing...  68.9 us

profile of v2, /device:TPU:0, one launch (start us, length us, event | category | flops | bytes accessed | tf_op | source)
XLA Modules:
  0.0 70.1 jit_solution(4495378810304222416)
XLA Ops:
  0.0 68.9 %shard_map.64 = f32[1,3,8,128,128]{4,3,2,1,0:T(8,128)S(1)} custom-call(f32[1,3,8,128,128]{4,3,2,1,0:T(8,128)} %f_hbm.1, f32[1,3,8,128,128]{4,3,2,1,0:T(8,128)} %k_hbm.1, f32[3,1,3]{2,1,0:T(1,128)} %bitcast.5, f32[3,1,3]{2,1,0:T(1,128)} %bitcast.6, s32[2,8]{1,0:T(2,128)} %bitcast.7, s32[3,8]{1,0:T(4,128)} %bitcast.4), custom_call_target="tpu_custom_call" | custom-call | tf_op jit(solution)/shard_map/pallas_call | solution.py:398
  68.9 1.1 %copy.8 = f32[1,3,8,128,128]{4,3,2,1,0:T(8,128)} copy(f32[1,3,8,128,128]{4,3,2,1,0:T(8,128)S(1)} %shard_map.64) | data formatting | bytes 3145728

commit v3 on v2

--- a/solution.py
+++ b/solution.py
@@ -29,7 +29,7 @@
     n_s, f_hbm, k_hbm, aniso_hbm, coup_hbm, levels_hbm, neigh_hbm, out,
     aniso, coup, levels, neigh,
     f, kk, kz, gx, gy, fz, rj, z0, w, q1, kzup, kza, kzb, up, za, zb, qup, qa, qb,
-    pu, ru, corr, rc, acc, mom, momr,
+    pu, ru0, ru1, ru2, corr, rc, acc, mom, momr,
     in_sem, ks, kr, zs, zr, qs, qr, ms, mr, ps, pr, cs, cr,
 ):
     g = lax.axis_index("grp")
@@ -38,6 +38,8 @@
     chunk = height // N_GRP
     below_id = (s + n_s - 1) % n_s
     above_id = (s + 1) % n_s
+
+    ru = (ru0, ru1, ru2)
 
     barrier = pltpu.get_barrier_semaphore()
     for o in range(1, n_s):
@@ -142,23 +144,34 @@
 
     lax.fori_loop(1, 9, z_faces, 0)
 
-    def first(k, carry):
-        sum_z = fz[k] + fz[k + 1]
-        for c in range(3):
-            inverse = 1.0 / (rj[c, k] + cf[c][2] * sum_z)
-            rj[c, k] = inverse
-            fc = f[c, k]
-            zc = fc * inverse
-            z0[c, k + 1] = zc
-            acc[0] += fold8(fc * zc)
-        return carry
-
-    lax.fori_loop(0, 8, first, 0)
-    for c in range(3):
-        up[c] = top_row(lambda j: z0[c, j + 1])
+    def jacobi(c, k):
+        return f[c, k] * (1.0 / (rj[c, k] + cf[c][2] * (fz[k] + fz[k + 1])))
+
+    for c in range(3):
+        z0[c, 1] = jacobi(c, 0)
+        up[c] = jacobi(c, a - 1)
     z_halo = halo(z0.at[:, 1], up, za, zb, zs, zr)
     for cpy in z_halo:
         cpy.start()
+
+    def invert(k):
+        sum_z = fz[k] + fz[k + 1]
+        for c in range(3):
+            rj[c, k] = 1.0 / (rj[c, k] + cf[c][2] * sum_z)
+
+    def first(k, carry):
+        invert(k)
+        for c in range(3):
+            fc = f[c, k]
+            zc = fc * rj[c, k]
+            z0[c, k + 1] = zc
+            acc[0] += fold8(fc * zc)
+        return carry
+
+    invert(0)
+    for c in range(3):
+        acc[0] += fold8(f[c, 0] * z0[c, 1])
+    lax.fori_loop(1, 8, first, 0)
 
     def apply_row(u, base, c, k, values):
         uc = values[c]
@@ -185,26 +198,33 @@
         cpy.wait()
     for c in range(3):
         zb[c] = zb[c] * has_below
+        wc = w[c, 0] - cf[c][2] * (fz[0] * zb[c])
+        w[c, 0] = wc
+        q1[c, 1] = wc * rj[c, 0]
+    q_down = remote(q1.at[:, 1], qa, qs.at[0], qr.at[0], {"slab": below_id})
+    q_down.start()
+    for c in range(3):
         za[c] = za[c] * has_above
-        w[c, 0] -= cf[c][2] * (fz[0] * zb[c])
         for i, j in enumerate(ROWS_UP):
             w[c, j] -= (sel[i] * cf[c][2]) * (fz[j + 1] * za[c])
 
+    def sums_of(c, k, qc):
+        wc = w[c, k]
+        acc[1] += fold8(z0[c, k + 1] * wc)
+        acc[2] += fold8(wc * qc)
+
     def third(k, carry):
         for c in range(3):
-            wc = w[c, k]
-            qc = wc * rj[c, k]
+            qc = w[c, k] * rj[c, k]
             q1[c, k + 1] = qc
-            acc[1] += fold8(z0[c, k + 1] * wc)
-            acc[2] += fold8(wc * qc)
-        return carry
-
-    lax.fori_loop(0, 8, third, 0)
+            sums_of(c, k, qc)
+        return carry
+
+    for c in range(3):
+        sums_of(c, 0, q1[c, 1])
+    lax.fori_loop(1, 8, third, 0)
     for c in range(3):
         qup[c] = top_row(lambda j: q1[c, j + 1])
-    q_halo = halo(q1.at[:, 1], qup, qa, qb, qs, qr)
-    for cpy in q_halo:
-        cpy.start()
 
     full = (a == 8).astype(jnp.float32)
     part = 1.0 - full
@@ -212,19 +232,12 @@
     def rows_of(i):
         return pl.ds(pl.multiple_of(i * chunk, chunk), chunk)
 
-    def scatter(src, dst, ssem, rsem):
-        copies = []
-        for o, (dy, dx) in enumerate(OFFSETS):
-            to = peer_of(g, dy, dx)
-            copies.append(
-                remote(src.at[:, :, rows_of(to)], dst.at[g], ssem.at[o], rsem.at[o], {"grp": to})
-            )
-        return copies
-
-    def await_from(dst, ssem, rsem, o):
+    def await_from(dst, c, ssem, rsem, o):
         dy, dx = OFFSETS[o]
         source = peer_of(g, N_Y - dy, dx)
-        remote(dst.at[source], dst.at[source], ssem.at[o], rsem.at[o], {"grp": source}).wait_recv()
+        ref = dst(source, c)
+        remote(ref, ref, ssem.at[c, o], rsem.at[c, o], {"grp": source}).wait_recv()
+        return source
 
     def fourth(k, carry):
         values = [q1[c, k + 1] for c in range(3)]
@@ -233,15 +246,10 @@
         return carry
 
     lax.fori_loop(0, 8, fourth, 0)
-    for cpy in q_halo:
-        cpy.wait()
-    for c in range(3):
-        qb[c] = qb[c] * has_below
-        qa[c] = qa[c] * has_above
-        cross = q1[c, 1] * (fz[0] * qb[c])
-        for i, j in enumerate(ROWS_UP):
-            cross = cross + sel[i] * (q1[c, j + 1] * (fz[j + 1] * qa[c]))
-        acc[3] -= cf[c][2] * fold8(cross)
+    fz_top = top_row(lambda j: fz[j + 1]) * (2.0 * has_above)
+    q_down.wait()
+    for c in range(3):
+        acc[3] -= cf[c][2] * fold8(qup[c] * (fz_top * qa[c]))
 
     for i in range(4):
         mom[i : i + 1] = jnp.sum(acc[i], axis=0, keepdims=True)
@@ -252,7 +260,8 @@
         m_out.append(remote(mom, momr.at[s], ms.at[o - 1], mr.at[o - 1], {"slab": to}))
     for cpy in m_out:
         cpy.start()
-
+    q_up = remote(qup, qb, qs.at[1], qr.at[1], {"slab": above_id})
+    q_up.start()
     momr[s] = mom[...]
     for o in range(1, n_s):
         source = (s + n_s - o) % n_s
@@ -272,12 +281,12 @@
     on_z = jnp.broadcast_to(step0 + step1 * (1.0 + beta), (height, width))
     on_q = jnp.broadcast_to(-step1 * step0, (height, width))
 
-    def solve(c, carry):
+    q_up.wait()
+    p_out = []
+    for c in range(3):
         rows = [on_z * z0[c, k + 1] + on_q * q1[c, k + 1] for k in range(8)]
-        rim_below = on_z * zb[c] + on_q * qb[c]
-        rim_above = on_z * za[c] + on_q * qa[c]
-        for k in range(8):
-            out[0, c, k] = rows[k]
+        rim_below = on_z * zb[c] + on_q * (qb[c] * has_below)
+        rim_above = on_z * za[c] + on_q * (qa[c] * has_above)
         for r in range(6):
             if r == 0:
                 value = part * rim_below
@@ -290,22 +299,23 @@
             if r < 4:
                 value = value + full * (rows[r] + pltpu.roll(rows[r + 4], width // 2, 1))
             pu[c, r] = value
-        return carry
-
-    lax.fori_loop(0, 3, solve, 0)
-    p_out = scatter(pu, ru, ps, pr)
-    for cpy in p_out:
-        cpy.start()
-    ru[g] = pu[:, :, rows_of(g)]
-    for o in range(len(OFFSETS)):
-        await_from(ru, ps, pr, o)
+        for o, (dy, dx) in enumerate(OFFSETS):
+            to = peer_of(g, dy, dx)
+            cpy = remote(
+                pu.at[c, :, rows_of(to)], ru[c].at[g], ps.at[c, o], pr.at[c, o], {"grp": to}
+            )
+            cpy.start()
+            p_out.append(cpy)
+        for k in range(8):
+            out[0, c, k] = rows[k]
+        ru[c][g] = pu[c, :, rows_of(g)]
 
     lanes = lax.broadcasted_iota(jnp.int32, (chunk, width), 1)
     half = lanes // 2
     beside = jnp.where(lanes % 2 == 1, half + 1, half + (width - 1)) % width
     low = (lanes < width // 2).astype(jnp.float32)
 
-    def mix(t):
+    def mix(t, c):
         lx, lz = levels[0, t], levels[1, t]
         nx_t, a_t = sizes(lx, lz)
         ids = [neigh[i, t] for i in range(3)]
@@ -315,49 +325,41 @@
         near = full_t * there[0]
         far = (1.0 - full_t) * there[0]
         on_x = (lanes < nx_t).astype(jnp.float32)
-
-        def one(c, carry):
-            for k in range(8):
-                m = k // 2
-                other = m + 2 * (k % 2)
-                if k < 4:
-                    v = near * ru[n0, c, k] + far * ru[n0, c, k + 1]
-                else:
-                    v = near * pltpu.roll(ru[n0, c, k - 4], width // 2, 1)
-                v = v * low
-                v = v - there[2] * (0.75 * ru[n2, c, m + 1] + 0.25 * ru[n2, c, other])
-                x = 0.75 * jnp.take_along_axis(v, half, axis=1) + 0.25 * jnp.take_along_axis(
-                    v, beside, axis=1
-                )
-                x = x + there[1] * (0.75 * ru[n1, c, m + 1] + 0.25 * ru[n1, c, other])
-                corr[t, c, k] = x * (on_x * (k < a_t).astype(jnp.float32))
-            return carry
-
-        lax.fori_loop(0, 3, one, 0)
+        for k in range(8):
+            m = k // 2
+            other = m + 2 * (k % 2)
+            if k < 4:
+                v = near * ru[c][n0, k] + far * ru[c][n0, k + 1]
+            else:
+                v = near * pltpu.roll(ru[c][n0, k - 4], width // 2, 1)
+            v = v * low
+            v = v - there[2] * (0.75 * ru[c][n2, m + 1] + 0.25 * ru[c][n2, other])
+            x = 0.75 * jnp.take_along_axis(v, half, axis=1) + 0.25 * jnp.take_along_axis(
+                v, beside, axis=1
+            )
+            x = x + there[1] * (0.75 * ru[c][n1, m + 1] + 0.25 * ru[c][n1, other])
+            corr[t, c, k] = x * (on_x * (k < a_t).astype(jnp.float32))
+
+    def finish(source, c, ref):
+        rows = rows_of(source)
+        for k in range(8):
+            out[0, c, k, rows] = out[0, c, k, rows] - ref[source, c, k]
 
     c_out = []
-    for o, (dy, dx) in enumerate(OFFSETS):
-        to = peer_of(g, dy, dx)
-        mix(to)
-        cpy = remote(corr.at[to], rc.at[g], cs.at[o], cr.at[o], {"grp": to})
-        cpy.start()
-        c_out.append(cpy)
-    mix(g)
-
-    def finish(source, ref):
-        rows = rows_of(source)
-
-        def one(k, carry):
-            for c in range(3):
-                out[0, c, k, rows] = out[0, c, k, rows] - ref[source, c, k]
-            return carry
-
-        lax.fori_loop(0, 8, one, 0)
-
-    finish(g, corr)
-    for o, (dy, dx) in enumerate(OFFSETS):
-        await_from(rc, cs, cr, o)
-        finish(peer_of(g, N_Y - dy, dx), rc)
+    for c in range(3):
+        for o in range(len(OFFSETS)):
+            await_from(lambda i, j: ru[j].at[i], c, ps, pr, o)
+        for o, (dy, dx) in enumerate(OFFSETS):
+            to = peer_of(g, dy, dx)
+            mix(to, c)
+            cpy = remote(corr.at[to, c], rc.at[g, c], cs.at[c, o], cr.at[c, o], {"grp": to})
+            cpy.start()
+            c_out.append(cpy)
+        mix(g, c)
+        finish(g, c, corr)
+    for c in range(3):
+        for o in range(len(OFFSETS)):
+            finish(await_from(lambda i, j: rc.at[i, j], c, cs, cr, o), c, rc)
     for cpy in m_out + p_out + c_out:
         cpy.wait_send()
 
@@ -387,13 +389,13 @@
             vm(*plane), vm(*plane), vm(*plane),
             vm(3, *plane), vm(3, *plane), vm(3, *plane),
             vm(3, *plane), vm(3, *plane), vm(3, *plane),
-            vm(3, 6, *plane), vm(N_GRP, 3, 6, chunk, width),
+            vm(3, 6, *plane), *(vm(N_GRP, 6, chunk, width) for _ in range(3)),
             vm(N_GRP, 3, 8, chunk, width), vm(N_GRP, 3, 8, chunk, width),
             vm(4, 8, width), vm(8, width), vm(n_s, 8, width),
             dma((6,)),
             dma((2,)), dma((2,)), dma((2,)), dma((2,)), dma((2,)), dma((2,)),
             dma((n_s - 1,)), dma((n_s - 1,)),
-            dma((others,)), dma((others,)), dma((others,)), dma((others,)),
+            dma((3, others)), dma((3, others)), dma((3, others)), dma((3, others)),
         ]
         return pl.pallas_call(
             functools.partial(body, n_s),

time: 70.5 us -> 65.4 us (0.928)
  Pallas kernels: 68.9 us -> 64.2 us
    pallas_call x1, Pallas kernels: 68.9 us -> 64.2 us  [per_device(): pl.pallas_call(functools.partial(body, n_s), out_shape=pltpu.VMEM(forcing...]
where the time goes in v3:
time: 65.4 us; the launch traced here: 65.3 us
  Pallas kernels  64.2 us (98%)
  local copies, waits for them, and re-layouts  1.15 us (2%)
    pallas_call x1, Pallas kernels, per_device(): pl.pallas_call(functools.partial(body, n_s), out_shape=pltpu.VMEM(forcing...  64.2 us

profile of v3, /device:TPU:0, one launch (start us, length us, event | category | flops | bytes accessed | tf_op | source)
XLA Modules:
  0.0 65.3 jit_solution(10601976059294526042)
XLA Ops:
  0.0 64.2 %shard_map.64 = f32[1,3,8,128,128]{4,3,2,1,0:T(8,128)S(1)} custom-call(f32[1,3,8,128,128]{4,3,2,1,0:T(8,128)} %f_hbm.1, f32[1,3,8,128,128]{4,3,2,1,0:T(8,128)} %k_hbm.1, f32[3,1,3]{2,1,0:T(1,128)} %bitcast.5, f32[3,1,3]{2,1,0:T(1,128)} %bitcast.6, s32[2,8]{1,0:T(2,128)} %bitcast.7, s32[3,8]{1,0:T(4,128)} %bitcast.4), custom_call_target="tpu_custom_call" | custom-call | tf_op jit(solution)/shard_map/pallas_call | solution.py:400
  64.2 1.1 %copy.8 = f32[1,3,8,128,128]{4,3,2,1,0:T(8,128)} copy(f32[1,3,8,128,128]{4,3,2,1,0:T(8,128)S(1)} %shard_map.64) | data formatting | bytes 3145728

commit v4 on v3

--- a/solution.py
+++ b/solution.py
@@ -29,8 +29,8 @@
     n_s, f_hbm, k_hbm, aniso_hbm, coup_hbm, levels_hbm, neigh_hbm, out,
     aniso, coup, levels, neigh,
     f, kk, kz, gx, gy, fz, rj, z0, w, q1, kzup, kza, kzb, up, za, zb, qup, qa, qb,
-    pu, ru0, ru1, ru2, corr, rc, acc, mom, momr,
-    in_sem, ks, kr, zs, zr, qs, qr, ms, mr, ps, pr, cs, cr,
+    pu, rim, rims, ru0, ru1, ru2, si0, si1, si2, ri0, ri1, ri2, corr, rc, acc, mom, momr,
+    in_sem, ks, kr, zs, zr, qs, qr, ms, mr, ps, pr, rs, rr, ds, dr, cs, cr,
 ):
     g = lax.axis_index("grp")
     s = lax.axis_index("slab")
@@ -40,6 +40,8 @@
     above_id = (s + 1) % n_s
 
     ru = (ru0, ru1, ru2)
+    inner_out = (si0, si1, si2)
+    inner = (ri0, ri1, ri2)
 
     barrier = pltpu.get_barrier_semaphore()
     for o in range(1, n_s):
@@ -227,16 +229,15 @@
         qup[c] = top_row(lambda j: q1[c, j + 1])
 
     full = (a == 8).astype(jnp.float32)
-    part = 1.0 - full
 
     def rows_of(i):
         return pl.ds(pl.multiple_of(i * chunk, chunk), chunk)
 
-    def await_from(dst, c, ssem, rsem, o):
+    def await_from(dst, ssem, rsem, c, o):
         dy, dx = OFFSETS[o]
         source = peer_of(g, N_Y - dy, dx)
         ref = dst(source, c)
-        remote(ref, ref, ssem.at[c, o], rsem.at[c, o], {"grp": source}).wait_recv()
+        remote(ref, ref, ssem.at[o], rsem.at[o], {"grp": source}).wait_recv()
         return source
 
     def fourth(k, carry):
@@ -281,34 +282,34 @@
     on_z = jnp.broadcast_to(step0 + step1 * (1.0 + beta), (height, width))
     on_q = jnp.broadcast_to(-step1 * step0, (height, width))
 
-    q_up.wait()
     p_out = []
-    for c in range(3):
-        rows = [on_z * z0[c, k + 1] + on_q * q1[c, k + 1] for k in range(8)]
-        rim_below = on_z * zb[c] + on_q * (qb[c] * has_below)
-        rim_above = on_z * za[c] + on_q * (qa[c] * has_above)
-        for r in range(6):
-            if r == 0:
-                value = part * rim_below
-            elif r == 3:
-                value = part * (rows[2] + sel[0] * rim_above)
-            elif r == 5:
-                value = sel[1] * rim_above
-            else:
-                value = part * rows[r - 1]
-            if r < 4:
-                value = value + full * (rows[r] + pltpu.roll(rows[r + 4], width // 2, 1))
-            pu[c, r] = value
+
+    def spread(src, dst, ssem, rsem):
         for o, (dy, dx) in enumerate(OFFSETS):
             to = peer_of(g, dy, dx)
-            cpy = remote(
-                pu.at[c, :, rows_of(to)], ru[c].at[g], ps.at[c, o], pr.at[c, o], {"grp": to}
-            )
+            cpy = remote(src(rows_of(to)), dst, ssem.at[o], rsem.at[o], {"grp": to})
             cpy.start()
             p_out.append(cpy)
+
+    odd = s % 2
+    is_odd = odd.astype(jnp.float32)
+    is_even = 1.0 - is_odd
+    for c in range(3):
+        if c == 2:
+            q_up.wait()
+            for e in range(3):
+                rim_below = on_z * zb[e] + on_q * (qb[e] * has_below)
+                rim_above = on_z * za[e] + on_q * (qa[e] * has_above)
+                rim[e] = is_even * rim_below + is_odd * rim_above
+            spread(lambda rows: rim.at[:, rows], rims.at[g], rs, rr)
+        solved = [on_z * z0[c, k + 1] + on_q * q1[c, k + 1] for k in range(8)]
+        for r in range(4):
+            pu[c, r] = solved[r] + full * pltpu.roll(solved[r + 4], width // 2, 1)
+        spread(lambda rows: pu.at[c, :, rows], ru[c].at[g], ps.at[c], pr.at[c])
         for k in range(8):
-            out[0, c, k] = rows[k]
+            out[0, c, k] = solved[k]
         ru[c][g] = pu[c, :, rows_of(g)]
+    rims[g] = rim[:, rows_of(g)]
 
     lanes = lax.broadcasted_iota(jnp.int32, (chunk, width), 1)
     half = lanes // 2
@@ -321,23 +322,37 @@
         ids = [neigh[i, t] for i in range(3)]
         there = [(i >= 0).astype(jnp.float32) for i in ids]
         n0, n1, n2 = (jnp.maximum(i, 0) for i in ids)
-        full_t = (a_t == 8).astype(jnp.float32)
-        near = full_t * there[0]
-        far = (1.0 - full_t) * there[0]
+        full_t = (a_t == 8).astype(jnp.float32) * there[0]
+        short = (a_t == 4).astype(jnp.float32)
         on_x = (lanes < nx_t).astype(jnp.float32)
+
+        def between(n):
+            ends = rims[n, c]
+            joint = inner[c][n]
+            below = is_even * ends + is_odd * joint
+            above = is_even * joint + is_odd * ends
+            near = [ru[c][n, k] for k in range(4)]
+            beyond = [below] + near + [above]
+            beyond[3] = near[2] + short * above
+            result = []
+            for k in range(8):
+                m = k // 2
+                other = near[m - 1] if k % 2 == 0 and m > 0 else beyond[m + 2 * (k % 2)]
+                result.append(0.75 * near[m] + 0.25 * other)
+            return result
+
+        across = between(n1)
+        both = between(n2)
         for k in range(8):
-            m = k // 2
-            other = m + 2 * (k % 2)
             if k < 4:
-                v = near * ru[c][n0, k] + far * ru[c][n0, k + 1]
+                v = there[0] * ru[c][n0, k]
             else:
-                v = near * pltpu.roll(ru[c][n0, k - 4], width // 2, 1)
-            v = v * low
-            v = v - there[2] * (0.75 * ru[c][n2, m + 1] + 0.25 * ru[c][n2, other])
+                v = full_t * pltpu.roll(ru[c][n0, k - 4], width // 2, 1)
+            v = v * low - there[2] * both[k]
             x = 0.75 * jnp.take_along_axis(v, half, axis=1) + 0.25 * jnp.take_along_axis(
                 v, beside, axis=1
             )
-            x = x + there[1] * (0.75 * ru[c][n1, m + 1] + 0.25 * ru[c][n1, other])
+            x = x + there[1] * across[k]
             corr[t, c, k] = x * (on_x * (k < a_t).astype(jnp.float32))
 
     def finish(source, c, ref):
@@ -348,7 +363,18 @@
     c_out = []
     for c in range(3):
         for o in range(len(OFFSETS)):
-            await_from(lambda i, j: ru[j].at[i], c, ps, pr, o)
+            await_from(lambda i, j: ru[j].at[i], ps.at[c], pr.at[c], c, o)
+        for p in range(N_GRP):
+            run = sizes(levels[0, p], levels[1, p])[1]
+            top = (run == 4).astype(jnp.float32)
+            last = top * ru[c][p, 3] + (1.0 - top) * ru[c][p, 1]
+            inner_out[c][p] = is_even * last + is_odd * ru[c][p, 0]
+        swap = remote(inner_out[c], inner[c], ds.at[c], dr.at[c], {"slab": s + 1 - 2 * odd})
+        swap.start()
+        if c == 0:
+            for o in range(len(OFFSETS)):
+                await_from(lambda i, j: rims.at[i], rs, rr, c, o)
+        swap.wait()
         for o, (dy, dx) in enumerate(OFFSETS):
             to = peer_of(g, dy, dx)
             mix(to, c)
@@ -359,7 +385,7 @@
         finish(g, c, corr)
     for c in range(3):
         for o in range(len(OFFSETS)):
-            finish(await_from(lambda i, j: rc.at[i, j], c, cs, cr, o), c, rc)
+            finish(await_from(lambda i, j: rc.at[i, j], cs.at[c], cr.at[c], c, o), c, rc)
     for cpy in m_out + p_out + c_out:
         cpy.wait_send()
 
@@ -389,13 +415,16 @@
             vm(*plane), vm(*plane), vm(*plane),
             vm(3, *plane), vm(3, *plane), vm(3, *plane),
             vm(3, *plane), vm(3, *plane), vm(3, *plane),
-            vm(3, 6, *plane), *(vm(N_GRP, 6, chunk, width) for _ in range(3)),
+            vm(3, 4, *plane), vm(3, *plane), vm(N_GRP, 3, chunk, width),
+            *(vm(N_GRP, 4, chunk, width) for _ in range(3)),
+            *(vm(N_GRP, chunk, width) for _ in range(6)),
             vm(N_GRP, 3, 8, chunk, width), vm(N_GRP, 3, 8, chunk, width),
             vm(4, 8, width), vm(8, width), vm(n_s, 8, width),
             dma((6,)),
             dma((2,)), dma((2,)), dma((2,)), dma((2,)), dma((2,)), dma((2,)),
             dma((n_s - 1,)), dma((n_s - 1,)),
-            dma((3, others)), dma((3, others)), dma((3, others)), dma((3, others)),
+            dma((3, others)), dma((3, others)), dma((others,)), dma((others,)), dma((3,)), dma((3,)),
+            dma((3, others)), dma((3, others)),
         ]
         return pl.pallas_call(
             functools.partial(body, n_s),

time: 65.4 us -> 63 us (0.963)
  Pallas kernels: 64.2 us -> 61.7 us
    pallas_call x1, Pallas kernels: 64.2 us -> 61.7 us  [per_device(): pl.pallas_call(functools.partial(body, n_s), out_shape=pltpu.VMEM(forcing...]
where the time goes in v4:
time: 63 us; the launch traced here: 62.9 us
  Pallas kernels  61.7 us (98%)
  local copies, waits for them, and re-layouts  1.15 us (2%)
    pallas_call x1, Pallas kernels, per_device(): pl.pallas_call(functools.partial(body, n_s), out_shape=pltpu.VMEM(forcing...  61.7 us

profile of v4, /device:TPU:0, one launch (start us, length us, event | category | flops | bytes accessed | tf_op | source)
XLA Modules:
  0.0 62.9 jit_solution(7903377230903569689)
XLA Ops:
  0.0 61.7 %shard_map.64 = f32[1,3,8,128,128]{4,3,2,1,0:T(8,128)S(1)} custom-call(f32[1,3,8,128,128]{4,3,2,1,0:T(8,128)} %f_hbm.1, f32[1,3,8,128,128]{4,3,2,1,0:T(8,128)} %k_hbm.1, f32[3,1,3]{2,1,0:T(1,128)} %bitcast.5, f32[3,1,3]{2,1,0:T(1,128)} %bitcast.6, s32[2,8]{1,0:T(2,128)} %bitcast.7, s32[3,8]{1,0:T(4,128)} %bitcast.4), custom_call_target="tpu_custom_call" | custom-call | tf_op jit(solution)/shard_map/pallas_call | solution.py:429
  61.7 1.1 %copy.8 = f32[1,3,8,128,128]{4,3,2,1,0:T(8,128)} copy(f32[1,3,8,128,128]{4,3,2,1,0:T(8,128)S(1)} %shard_map.64) | data formatting | bytes 3145728

commit v5 on v4

--- a/solution.py
+++ b/solution.py
@@ -254,7 +254,6 @@
 
     for i in range(4):
         mom[i : i + 1] = jnp.sum(acc[i], axis=0, keepdims=True)
-    mom[4:8] = jnp.zeros((4, width), jnp.float32)
     m_out = []
     for o in range(1, n_s):
         to = (s + o) % n_s
@@ -360,7 +359,15 @@
         for k in range(8):
             out[0, c, k, rows] = out[0, c, k, rows] - ref[source, c, k]
 
-    c_out = []
+    def answer_copy(c, o):
+        to = peer_of(g, o // 2, o % 2)
+        return remote(corr.at[to, c], rc.at[g, c], cs.at[c, o - 1], cr.at[c, o - 1], {"grp": to})
+
+    def end_answer(o, carry):
+        for c in range(3):
+            answer_copy(c, o).wait_send()
+        return carry
+
     for c in range(3):
         for o in range(len(OFFSETS)):
             await_from(lambda i, j: ru[j].at[i], ps.at[c], pr.at[c], c, o)
@@ -375,18 +382,26 @@
             for o in range(len(OFFSETS)):
                 await_from(lambda i, j: rims.at[i], rs, rr, c, o)
         swap.wait()
-        for o, (dy, dx) in enumerate(OFFSETS):
-            to = peer_of(g, dy, dx)
+
+        def answer(o, carry):
+            to = peer_of(g, o // 2, o % 2)
             mix(to, c)
-            cpy = remote(corr.at[to, c], rc.at[g, c], cs.at[c, o], cr.at[c, o], {"grp": to})
-            cpy.start()
-            c_out.append(cpy)
+            answer_copy(c, o).start()
+            return carry
+
+        lax.fori_loop(1, N_GRP, answer, 0)
         mix(g, c)
         finish(g, c, corr)
     for c in range(3):
         for o in range(len(OFFSETS)):
-            finish(await_from(lambda i, j: rc.at[i, j], cs.at[c], cr.at[c], c, o), c, rc)
-    for cpy in m_out + p_out + c_out:
+            dy, dx = OFFSETS[o]
+            source = peer_of(g, N_Y - dy, dx)
+            ref = rc.at[source, c]
+            i = 2 * dy + dx - 1
+            remote(ref, ref, cs.at[c, i], cr.at[c, i], {"grp": source}).wait_recv()
+            finish(source, c, rc)
+    lax.fori_loop(1, N_GRP, end_answer, 0)
+    for cpy in m_out + p_out:
         cpy.wait_send()
 
 
@@ -419,7 +434,7 @@
             *(vm(N_GRP, 4, chunk, width) for _ in range(3)),
             *(vm(N_GRP, chunk, width) for _ in range(6)),
             vm(N_GRP, 3, 8, chunk, width), vm(N_GRP, 3, 8, chunk, width),
-            vm(4, 8, width), vm(8, width), vm(n_s, 8, width),
+            vm(4, 8, width), vm(4, width), vm(n_s, 4, width),
             dma((6,)),
             dma((2,)), dma((2,)), dma((2,)), dma((2,)), dma((2,)), dma((2,)),
             dma((n_s - 1,)), dma((n_s - 1,)),

time: 63 us -> 62.7 us (level)
  no operation moved by 1% of the time
where the time goes in v5:
time: 62.7 us; the launch traced here: 62.6 us
  Pallas kernels  61.5 us (98%)
  local copies, waits for them, and re-layouts  1.15 us (2%)
    pallas_call x1, Pallas kernels, per_device(): pl.pallas_call(functools.partial(body, n_s), out_shape=pltpu.VMEM(forcing...  61.5 us

profile of v5, /device:TPU:0, one launch (start us, length us, event | category | flops | bytes accessed | tf_op | source)
XLA Modules:
  0.0 62.6 jit_solution(1836655121218424213)
XLA Ops:
  0.0 61.5 %shard_map.64 = f32[1,3,8,128,128]{4,3,2,1,0:T(8,128)S(1)} custom-call(f32[1,3,8,128,128]{4,3,2,1,0:T(8,128)} %f_hbm.1, f32[1,3,8,128,128]{4,3,2,1,0:T(8,128)} %k_hbm.1, f32[3,1,3]{2,1,0:T(1,128)} %bitcast.5, f32[3,1,3]{2,1,0:T(1,128)} %bitcast.6, s32[2,8]{1,0:T(2,128)} %bitcast.7, s32[3,8]{1,0:T(4,128)} %bitcast.4), custom_call_target="tpu_custom_call" | custom-call | tf_op jit(solution)/shard_map/pallas_call | solution.py:444
  61.5 1.1 %copy.8 = f32[1,3,8,128,128]{4,3,2,1,0:T(8,128)} copy(f32[1,3,8,128,128]{4,3,2,1,0:T(8,128)S(1)} %shard_map.64) | data formatting | bytes 3145728

commit v6 on v5

--- a/solution.py
+++ b/solution.py
@@ -383,7 +383,8 @@
                 await_from(lambda i, j: rims.at[i], rs, rr, c, o)
         swap.wait()
 
-        def answer(o, carry):
+        def answer(i, carry):
+            o = 1 + (i * (3 + 2 * odd) + 6) % 7
             to = peer_of(g, o // 2, o % 2)
             mix(to, c)
             answer_copy(c, o).start()

time: 62.7 us -> 63.7 us (1.016); the launches traced: 62.6 us -> 62.6 us
  no operation moved by 1% of the time
where the time goes in v6:
time: 63.7 us; the launch traced here: 62.6 us
  Pallas kernels  61.5 us (97%)
  local copies, waits for them, and re-layouts  1.15 us (2%)
    pallas_call x1, Pallas kernels, per_device(): pl.pallas_call(functools.partial(body, n_s), out_shape=pltpu.VMEM(forcing...  61.5 us

profile of v6, /device:TPU:0, one launch (start us, length us, event | category | flops | bytes accessed | tf_op | source)
XLA Modules:
  0.0 62.6 jit_solution(5168946920661118664)
XLA Ops:
  0.0 61.5 %shard_map.64 = f32[1,3,8,128,128]{4,3,2,1,0:T(8,128)S(1)} custom-call(f32[1,3,8,128,128]{4,3,2,1,0:T(8,128)} %f_hbm.1, f32[1,3,8,128,128]{4,3,2,1,0:T(8,128)} %k_hbm.1, f32[3,1,3]{2,1,0:T(1,128)} %bitcast.5, f32[3,1,3]{2,1,0:T(1,128)} %bitcast.6, s32[2,8]{1,0:T(2,128)} %bitcast.7, s32[3,8]{1,0:T(4,128)} %bitcast.4), custom_call_target="tpu_custom_call" | custom-call | tf_op jit(solution)/shard_map/pallas_call | solution.py:445
  61.5 1.1 %copy.8 = f32[1,3,8,128,128]{4,3,2,1,0:T(8,128)} copy(f32[1,3,8,128,128]{4,3,2,1,0:T(8,128)S(1)} %shard_map.64) | data formatting | bytes 3145728
